TPU v7x, 32 devices: a whole 2x2x4 slice. The times are simulated.
32 devices in a mesh: study: 2 (over x), ky: 16 (over z, y, core).
Axes of the slice: x: 2, y: 2, z: 4, core: 2. Of those that a mesh axis runs over, the one named last changes fastest.
Arguments:
- kspace: bfloat16 [32, 2, 32, 256, 256], P('study', None, None, 'ky'), parts along dimension 0, may hold values from -6 to 6
- kernel: bfloat16 [2, 768, 64], replicated, may hold values from -0.21875 to 0.21875
- pattern: int32 [32], P('study'), parts along dimension 0, may hold values from 0 to 2
- offsets: int32 [4], replicated, may hold values from -2 to 2
- segment: int32 [256], replicated, may hold values from 0 to 2
- temporal_basis: float32 [5, 16], replicated, may hold values from -1.5 to 1.5
Outputs:
- basis_images: float32 [10, 2, 32, 256, 256], P('study', None, None, 'ky'), parts along dimension 0
There are 2 independent parts, one for each index of `study`. A program takes and returns all parts, laid end to end along the dimension named above; an argument that names none is the same for every part. Nothing has to cross between parts.
All inputs are finite; a program needn't handle non-finite values.
Results may differ from a plain program's by a relative error of at most 0.0003.
Values may be sent and summed in bfloat16 or wider, within the bound.
No kernel may reach another device: no remote copies, remote signals or barrier semaphores. Data moves between devices by JAX's collectives and lax.ppermute only.
A program may use at most 192 MiB of HBM per device.

v0:
```python
import jax
import jax.numpy as jnp
from jax import lax
from jax.sharding import PartitionSpec as P

frame_block = 4


def padded_2(block, sides, width):
    for axis, dim in sides:
        count = lax.axis_size(axis)
        forward = [(i, i + 1) for i in range(count - 1)]
        backward = [(target, source) for source, target in forward]
        low = lax.ppermute(
            lax.slice_in_dim(block, block.shape[dim] - width, None, axis=dim), axis, forward
        )
        high = lax.ppermute(lax.slice_in_dim(block, 0, width, axis=dim), axis, backward)
        block = jnp.concatenate([low, block, high], axis=dim)
    return block


def inverse_rows(spectra):
    row_total = spectra.shape[3]
    row_index = jnp.arange(row_total, dtype=jnp.int32)
    phase_index = row_index[:, None] * row_index[None, :] % row_total
    phase_angle = phase_index.astype(jnp.float32) * (2.0 * jnp.pi / row_total)
    cosine_table = jnp.cos(phase_angle)
    sine_table = jnp.sin(phase_angle)
    real_part = spectra[:, 0]
    imag_part = spectra[:, 1]
    high = lax.Precision.HIGHEST
    out_real = jnp.einsum("yk,mckx->mcxy", cosine_table, real_part, precision=high) - jnp.einsum(
        "yk,mckx->mcxy", sine_table, imag_part, precision=high
    )
    out_imag = jnp.einsum("yk,mckx->mcxy", sine_table, real_part, precision=high) + jnp.einsum(
        "yk,mckx->mcxy", cosine_table, imag_part, precision=high
    )
    scale = 1.0 / jnp.sqrt(jnp.float32(row_total))
    return jnp.stack([out_real, out_imag], axis=1) * scale


def on_device(kspace, kernel, pattern, offsets, segment, temporal_basis):
    frame_total, _, coil_count, row_count, kx_count = kspace.shape
    group_count = kernel.shape[0]
    group_frames = frame_total // group_count
    row_start = lax.axis_index("ky") * row_count
    local_segment = lax.dynamic_slice_in_dim(segment, row_start, row_count)
    acquired = (local_segment[None, :] == pattern[:, None])[:, None, None, :, None]
    zero_fill = jnp.where(acquired, kspace, jnp.zeros_like(kspace))
    padded = padded_2(zero_fill, (("ky", 3),), 1)
    blocks = frame_total // frame_block
    padded_blocks = padded.reshape(blocks, frame_block, 2, coil_count, row_count + 2, kx_count)
    block_group = jnp.arange(blocks, dtype=jnp.int32) * frame_block // group_frames

    def estimate_block(block_item):
        block_data, group_index = block_item
        ky_layers = []
        for ky_tap in range(3):
            ky_slice = block_data[:, :, :, ky_tap : ky_tap + row_count, :]
            ky_layers.append(
                jnp.stack(
                    [
                        jnp.roll(ky_slice, -offsets[kx_tap], axis=4)
                        for kx_tap in range(offsets.shape[0])
                    ],
                    axis=2,
                )
            )
        sources = jnp.stack(ky_layers, axis=2).reshape(frame_block, -1, row_count * kx_count)
        weights = lax.dynamic_index_in_dim(kernel, group_index, 0, keepdims=False)
        return jnp.einsum("io,fir->for", weights, sources, preferred_element_type=jnp.float32)

    estimate = lax.map(estimate_block, (padded_blocks, block_group))
    estimate = estimate.reshape(frame_total, 2, coil_count, row_count, kx_count)
    filled = jnp.where(acquired, kspace.astype(jnp.float32), estimate)
    high = lax.Precision.HIGHEST
    coefficients = jnp.einsum("bf,fpcrx->bpcrx", temporal_basis, filled, precision=high)
    swapped = lax.all_to_all(coefficients, "ky", split_axis=4, concat_axis=3, tiled=True)
    return inverse_rows(swapped)


def solution(mesh):
    return jax.shard_map(
        on_device,
        mesh=mesh,
        in_specs=(P("study", None, None, "ky", None), P(), P("study"), P(), P(), P()),
        out_specs=P("study", None, None, "ky", None),
        check_vma=False,
    )
```

profile of v0, /device:TPU:1, one launch (start us, length us, event | category | flops | bytes accessed | tf_op | source)
XLA Modules:
  0.0 757.7 jit_solution(11994539295915836448)
XLA Ops:
  1.5 7.2 broadcast_select_fusion
  8.7 4.6 fusion.80
  13.5 4.5 collective-permute-start
  18.1 1.9 collective-permute-start.1
  23.3 6.4 collective-permute-done
  31.8 13.5 %pad_maximum_fusion.1 = bf16[16,2,32,18,256]{4,3,2,1,0:T(8,128)(2,1)} fusion(bf16[16,2,32,1,256]{4,3,2,1,0:T(2,128)(2,1)S(1)} %copy.40, bf16[16,2,32,16,256]{4,3,2,1,0:T(8,128)(2,1)} %broadcast_select_fusion, bf16[16,2,32,1,256]{4,3,2,1,0:T(2,128)(2,1)S(1)} %copy.39), kind=kLoop, calls=%fused_computation.61 | loop fusion | flops 28311552 | bytes 18874368 | tf_op jit(solution)/shard_map/concatenate | solution.py:18
  45.4 423.2 %while.12 = (s32[]{:T(128)}, f32[4,4,64,4096]{3,2,1,0:T(8,128)}, bf16[4,4,2,32,18,256]{5,4,3,2,1,0:T(8,128)(2,1)}, s32[]{:T(128)}, s32[]{:T(128)}, /*index=5*/s3...) while((s32[]{:T(128)}, f32[4,4,64,4096]{3,2,1,0:T(8,128)}, ...), condition=%wide.region_1.3_spmd, body=%wide.region_0.2_spmd.sunk | while | flops 1723858944 | bytes 229213552 | solution.py:73
  45.6 2.1 dynamic-slice_bitcast_fusion.2
  47.8 2.8 fusion.92
  50.6 7.1 fusion.94
  57.6 9.1 %fusion.95 = (bf16[4,2,1,32,16,256]{5,4,3,2,1,0:T(8,128)(2,1)}, bf16[4,2,1,32,16,256]{5,4,3,2,1,0:T(8,128)(2,1)}, bf16[4,2,1,32,16,256]{5,4,3,2,1,0:T(8,128)(2,1)}, bf16[4,2,1,32,16,256]{5,4,3,2,1,0:T(8,128)(2,1)}) fusion(s32[]{:T(128)S(6)} %select_n.129, bf16[4,2,32,16,256]{4,3,2,1,0:T(8,128)(2,1)S(1)} %get-tuple-element.228, s32[]{:T(128)S(6)} %select_n.131, ...), kind=kLoop, calls=%fused_computation.42.clone.1 | loop fusion | flops 16777216 | bytes 10485776 | tf_op jit(solution)/shard_map/while/body/eval_jaxpr/stack | solution.py:61
  66.7 5.8 maximum_bitcast_fusion.6
  72.6 12.3 %fusion.93 = (bf16[4,2,1,32,16,256]{5,4,3,2,1,0:T(8,128)(2,1)S(1)}, bf16[4,2,1,32,16,256]{5,4,3,2,1,0:T(8,128)(2,1)S(1)}, bf16[4,2,1,32,16,256]{5,4,3,2,1,0:T(8,128)(2,1)S(1)}, bf16[4,2,1,32,16,256]{5,4,3,2,1,0:T(8,128)(2,1)S(1)}) fusion(s32[]{:T(128)S(6)} %select_n.129, bf16[4,2,32,16,256]{4,3,2,1,0:T(8,128)(2,1)} %get-tuple-element.218, ...), kind=kLoop, calls=%fused_computation.34.clone.1 | loop fusion | flops 16777216 | bytes 10485776 | tf_op jit(solution)/shard_map/while/body/eval_jaxpr/stack | solution.py:61
  84.9 1.1 maximum_bitcast_fusion.5
  86.1 10.2 %pad_maximum_fusion.3 = bf16[4,2,3,4,32,16,256]{6,5,4,3,2,1,0:T(8,128)(2,1)} fusion(bf16[4,2,1,4,32,16,256]{6,5,4,3,2,1,0:T(8,128)(2,1)S(1)} %maximum_bitcast_fusion.5, bf16[4,2,1,4,32,16,256]{6,5,4,3,2,1,0:T(8,128)(2,1)S(1)} %get-tuple-element.233, bf16[4,2,1,4,32,16,256]{6,5,4,3,2,1,0:T(8,128)(2,1)S(1)} %get-tuple-element.234), kind=kLoop, calls=%fused_computation.clone.1 | loop fusion | flops 25165824 | bytes 50331648 | tf_op jit(solution)/shard_map/while/body/eval_jaxpr/stack | solution.py:69
  96.3 37.8 %reshape.50 = bf16[4,768,4096]{2,1,0:T(8,128)(2,1)} reshape(bf16[4,2,3,4,32,16,256]{6,5,4,3,2,1,0:T(8,128)(2,1)} %pad_maximum_fusion.3) | data formatting | bytes 50331648 | tf_op jit(solution)/shard_map/while/body/eval_jaxpr/reshape | solution.py:69
  136.6 14.8 %fusion.96 = f32[4,4,64,4096]{3,2,1,0:T(8,128)} fusion(f32[4,4,64,4096]{3,2,1,0:T(8,128)} %get-tuple-element.251, s32[]{:T(128)} %get-tuple-element.250, bf16[4,768,4096]{2,1,0:T(8,128)(2,1)} %reshape.50, bf16[2,768,64]{1,2,0:T(8,128)(2,1)S(1)} %get-tuple-element.273, s32[]{:T(128)S(6)} %select_n.136), kind=kOutput, calls=%fused_computation.29.clone.1 | convolution fusion | flops 1610612736 | bytes 29458948 | tf_op jit(solution)/shard_map/while/body/eval_jaxpr/io,fir->for/dot_general | solution.py:71
  151.4 2.1 dynamic-slice_bitcast_fusion.2
  153.5 2.8 fusion.92
  156.3 7.1 fusion.94
  163.3 9.1 %fusion.95 = (bf16[4,2,1,32,16,256]{5,4,3,2,1,0:T(8,128)(2,1)}, bf16[4,2,1,32,16,256]{5,4,3,2,1,0:T(8,128)(2,1)}, bf16[4,2,1,32,16,256]{5,4,3,2,1,0:T(8,128)(2,1)}, bf16[4,2,1,32,16,256]{5,4,3,2,1,0:T(8,128)(2,1)}) fusion(s32[]{:T(128)S(6)} %select_n.129, bf16[4,2,32,16,256]{4,3,2,1,0:T(8,128)(2,1)S(1)} %get-tuple-element.228, s32[]{:T(128)S(6)} %select_n.131, ...), kind=kLoop, calls=%fused_computation.42.clone.1 | loop fusion | flops 16777216 | bytes 10485776 | tf_op jit(solution)/shard_map/while/body/eval_jaxpr/stack | solution.py:61
  172.5 5.8 maximum_bitcast_fusion.6
  178.3 12.3 %fusion.93 = (bf16[4,2,1,32,16,256]{5,4,3,2,1,0:T(8,128)(2,1)S(1)}, bf16[4,2,1,32,16,256]{5,4,3,2,1,0:T(8,128)(2,1)S(1)}, bf16[4,2,1,32,16,256]{5,4,3,2,1,0:T(8,128)(2,1)S(1)}, bf16[4,2,1,32,16,256]{5,4,3,2,1,0:T(8,128)(2,1)S(1)}) fusion(s32[]{:T(128)S(6)} %select_n.129, bf16[4,2,32,16,256]{4,3,2,1,0:T(8,128)(2,1)} %get-tuple-element.218, ...), kind=kLoop, calls=%fused_computation.34.clone.1 | loop fusion | flops 16777216 | bytes 10485776 | tf_op jit(solution)/shard_map/while/body/eval_jaxpr/stack | solution.py:61
  190.6 1.1 maximum_bitcast_fusion.5
  191.8 10.2 %pad_maximum_fusion.3 = bf16[4,2,3,4,32,16,256]{6,5,4,3,2,1,0:T(8,128)(2,1)} fusion(bf16[4,2,1,4,32,16,256]{6,5,4,3,2,1,0:T(8,128)(2,1)S(1)} %maximum_bitcast_fusion.5, bf16[4,2,1,4,32,16,256]{6,5,4,3,2,1,0:T(8,128)(2,1)S(1)} %get-tuple-element.233, bf16[4,2,1,4,32,16,256]{6,5,4,3,2,1,0:T(8,128)(2,1)S(1)} %get-tuple-element.234), kind=kLoop, calls=%fused_computation.clone.1 | loop fusion | flops 25165824 | bytes 50331648 | tf_op jit(solution)/shard_map/while/body/eval_jaxpr/stack | solution.py:69
  202.0 37.8 %reshape.50 = bf16[4,768,4096]{2,1,0:T(8,128)(2,1)} reshape(bf16[4,2,3,4,32,16,256]{6,5,4,3,2,1,0:T(8,128)(2,1)} %pad_maximum_fusion.3) | data formatting | bytes 50331648 | tf_op jit(solution)/shard_map/while/body/eval_jaxpr/reshape | solution.py:69
  242.3 14.7 %fusion.96 = f32[4,4,64,4096]{3,2,1,0:T(8,128)} fusion(f32[4,4,64,4096]{3,2,1,0:T(8,128)} %get-tuple-element.251, s32[]{:T(128)} %get-tuple-element.250, bf16[4,768,4096]{2,1,0:T(8,128)(2,1)} %reshape.50, bf16[2,768,64]{1,2,0:T(8,128)(2,1)S(1)} %get-tuple-element.273, s32[]{:T(128)S(6)} %select_n.136), kind=kOutput, calls=%fused_computation.29.clone.1 | convolution fusion | flops 1610612736 | bytes 29458948 | tf_op jit(solution)/shard_map/while/body/eval_jaxpr/io,fir->for/dot_general | solution.py:71
  257.0 2.1 dynamic-slice_bitcast_fusion.2
  259.1 2.8 fusion.92
  261.9 7.1 fusion.94
  269.0 9.1 %fusion.95 = (bf16[4,2,1,32,16,256]{5,4,3,2,1,0:T(8,128)(2,1)}, bf16[4,2,1,32,16,256]{5,4,3,2,1,0:T(8,128)(2,1)}, bf16[4,2,1,32,16,256]{5,4,3,2,1,0:T(8,128)(2,1)}, bf16[4,2,1,32,16,256]{5,4,3,2,1,0:T(8,128)(2,1)}) fusion(s32[]{:T(128)S(6)} %select_n.129, bf16[4,2,32,16,256]{4,3,2,1,0:T(8,128)(2,1)S(1)} %get-tuple-element.228, s32[]{:T(128)S(6)} %select_n.131, ...), kind=kLoop, calls=%fused_computation.42.clone.1 | loop fusion | flops 16777216 | bytes 10485776 | tf_op jit(solution)/shard_map/while/body/eval_jaxpr/stack | solution.py:61
  278.1 5.8 maximum_bitcast_fusion.6
  283.9 12.3 %fusion.93 = (bf16[4,2,1,32,16,256]{5,4,3,2,1,0:T(8,128)(2,1)S(1)}, bf16[4,2,1,32,16,256]{5,4,3,2,1,0:T(8,128)(2,1)S(1)}, bf16[4,2,1,32,16,256]{5,4,3,2,1,0:T(8,128)(2,1)S(1)}, bf16[4,2,1,32,16,256]{5,4,3,2,1,0:T(8,128)(2,1)S(1)}) fusion(s32[]{:T(128)S(6)} %select_n.129, bf16[4,2,32,16,256]{4,3,2,1,0:T(8,128)(2,1)} %get-tuple-element.218, ...), kind=kLoop, calls=%fused_computation.34.clone.1 | loop fusion | flops 16777216 | bytes 10485776 | tf_op jit(solution)/shard_map/while/body/eval_jaxpr/stack | solution.py:61
  296.3 1.1 maximum_bitcast_fusion.5
  297.4 10.2 %pad_maximum_fusion.3 = bf16[4,2,3,4,32,16,256]{6,5,4,3,2,1,0:T(8,128)(2,1)} fusion(bf16[4,2,1,4,32,16,256]{6,5,4,3,2,1,0:T(8,128)(2,1)S(1)} %maximum_bitcast_fusion.5, bf16[4,2,1,4,32,16,256]{6,5,4,3,2,1,0:T(8,128)(2,1)S(1)} %get-tuple-element.233, bf16[4,2,1,4,32,16,256]{6,5,4,3,2,1,0:T(8,128)(2,1)S(1)} %get-tuple-element.234), kind=kLoop, calls=%fused_computation.clone.1 | loop fusion | flops 25165824 | bytes 50331648 | tf_op jit(solution)/shard_map/while/body/eval_jaxpr/stack | solution.py:69
  307.6 37.8 %reshape.50 = bf16[4,768,4096]{2,1,0:T(8,128)(2,1)} reshape(bf16[4,2,3,4,32,16,256]{6,5,4,3,2,1,0:T(8,128)(2,1)} %pad_maximum_fusion.3) | data formatting | bytes 50331648 | tf_op jit(solution)/shard_map/while/body/eval_jaxpr/reshape | solution.py:69
  347.9 14.7 %fusion.96 = f32[4,4,64,4096]{3,2,1,0:T(8,128)} fusion(f32[4,4,64,4096]{3,2,1,0:T(8,128)} %get-tuple-element.251, s32[]{:T(128)} %get-tuple-element.250, bf16[4,768,4096]{2,1,0:T(8,128)(2,1)} %reshape.50, bf16[2,768,64]{1,2,0:T(8,128)(2,1)S(1)} %get-tuple-element.273, s32[]{:T(128)S(6)} %select_n.136), kind=kOutput, calls=%fused_computation.29.clone.1 | convolution fusion | flops 1610612736 | bytes 29458948 | tf_op jit(solution)/shard_map/while/body/eval_jaxpr/io,fir->for/dot_general | solution.py:71
  362.6 2.1 dynamic-slice_bitcast_fusion.2
  364.7 2.8 fusion.92
  367.5 7.1 fusion.94
  374.6 9.1 %fusion.95 = (bf16[4,2,1,32,16,256]{5,4,3,2,1,0:T(8,128)(2,1)}, bf16[4,2,1,32,16,256]{5,4,3,2,1,0:T(8,128)(2,1)}, bf16[4,2,1,32,16,256]{5,4,3,2,1,0:T(8,128)(2,1)}, bf16[4,2,1,32,16,256]{5,4,3,2,1,0:T(8,128)(2,1)}) fusion(s32[]{:T(128)S(6)} %select_n.129, bf16[4,2,32,16,256]{4,3,2,1,0:T(8,128)(2,1)S(1)} %get-tuple-element.228, s32[]{:T(128)S(6)} %select_n.131, ...), kind=kLoop, calls=%fused_computation.42.clone.1 | loop fusion | flops 16777216 | bytes 10485776 | tf_op jit(solution)/shard_map/while/body/eval_jaxpr/stack | solution.py:61
  383.7 5.8 maximum_bitcast_fusion.6
  389.5 12.3 %fusion.93 = (bf16[4,2,1,32,16,256]{5,4,3,2,1,0:T(8,128)(2,1)S(1)}, bf16[4,2,1,32,16,256]{5,4,3,2,1,0:T(8,128)(2,1)S(1)}, bf16[4,2,1,32,16,256]{5,4,3,2,1,0:T(8,128)(2,1)S(1)}, bf16[4,2,1,32,16,256]{5,4,3,2,1,0:T(8,128)(2,1)S(1)}) fusion(s32[]{:T(128)S(6)} %select_n.129, bf16[4,2,32,16,256]{4,3,2,1,0:T(8,128)(2,1)} %get-tuple-element.218, ...), kind=kLoop, calls=%fused_computation.34.clone.1 | loop fusion | flops 16777216 | bytes 10485776 | tf_op jit(solution)/shard_map/while/body/eval_jaxpr/stack | solution.py:61
  401.9 1.1 maximum_bitcast_fusion.5
  403.0 10.2 %pad_maximum_fusion.3 = bf16[4,2,3,4,32,16,256]{6,5,4,3,2,1,0:T(8,128)(2,1)} fusion(bf16[4,2,1,4,32,16,256]{6,5,4,3,2,1,0:T(8,128)(2,1)S(1)} %maximum_bitcast_fusion.5, bf16[4,2,1,4,32,16,256]{6,5,4,3,2,1,0:T(8,128)(2,1)S(1)} %get-tuple-element.233, bf16[4,2,1,4,32,16,256]{6,5,4,3,2,1,0:T(8,128)(2,1)S(1)} %get-tuple-element.234), kind=kLoop, calls=%fused_computation.clone.1 | loop fusion | flops 25165824 | bytes 50331648 | tf_op jit(solution)/shard_map/while/body/eval_jaxpr/stack | solution.py:69
  413.2 37.8 %reshape.50 = bf16[4,768,4096]{2,1,0:T(8,128)(2,1)} reshape(bf16[4,2,3,4,32,16,256]{6,5,4,3,2,1,0:T(8,128)(2,1)} %pad_maximum_fusion.3) | data formatting | bytes 50331648 | tf_op jit(solution)/shard_map/while/body/eval_jaxpr/reshape | solution.py:69
  453.5 14.7 %fusion.96 = f32[4,4,64,4096]{3,2,1,0:T(8,128)} fusion(f32[4,4,64,4096]{3,2,1,0:T(8,128)} %get-tuple-element.251, s32[]{:T(128)} %get-tuple-element.250, bf16[4,768,4096]{2,1,0:T(8,128)(2,1)} %reshape.50, bf16[2,768,64]{1,2,0:T(8,128)(2,1)S(1)} %get-tuple-element.273, s32[]{:T(128)S(6)} %select_n.136), kind=kOutput, calls=%fused_computation.29.clone.1 | convolution fusion | flops 1610612736 | bytes 29458948 | tf_op jit(solution)/shard_map/while/body/eval_jaxpr/io,fir->for/dot_general | solution.py:71
  468.6 11.0 %copy.54 = f32[128,8,16,256]{3,2,1,0:T(8,128)S(1)} copy(f32[128,8,16,256]{3,1,2,0:T(8,128)} %bitcast.126) | data formatting | bytes 33554432
  479.6 6.1 convert_select_fusion
  485.7 17.8 %fusion.30 = f32[5,2,32,16,256]{4,0,3,2,1:T(8,128)} fusion(f32[16,2,32,16,256]{4,3,2,1,0:T(8,128)S(1)} %convert_select_fusion, f32[5,16]{1,0:T(8,128)S(1)} %copy-done), kind=kOutput, calls=%fused_computation.64 | convolution fusion | flops 251658240 | bytes 22020416 | tf_op jit(solution)/shard_map/bf,fpcrx->bpcrx/dot_general | solution.py:77
  503.6 14.0 %copy.42 = f32[5,2,32,16,256]{2,3,1,0,4:T(8,128)} copy(f32[5,2,32,16,256]{4,0,3,2,1:T(8,128)} %fusion.30) | data formatting | bytes 10485760 | tf_op jit(solution)/shard_map/bf,fpcrx->bpcrx/dot_general | solution.py:77
  517.5 18.0 %reshape.47 = f32[16,1,81920]{2,1,0:T(1,128)} reshape(f32[256,5,2,16,32]{4,3,2,1,0:T(8,128)} %bitcast.122) | data formatting | bytes 10485760
  535.5 121.4 %all_to_all.18 = f32[16,1,81920]{2,1,0:T(1,128)} all-to-all(f32[16,1,81920]{2,1,0:T(1,128)} %reshape.47), channel_id=1, replica_groups=mesh['study'=2,'ky'=16] {'ky'}, dimensions={0} | all-to-all | bytes 10485760 | tf_op jit(solution)/shard_map/all_to_all | solution.py:78
  657.4 16.9 %reduce = f32[16,81920]{1,0:T(8,128)} reduce(f32[16,1,81920]{2,1,0:T(1,128)} %all_to_all.18, f32[]{:T(128)} %broadcast.61), dimensions={1}, to_apply=%all_to_all.13.reduce_sub_computation | reduce | bytes 10485764 | tf_op jit(solution)/shard_map/all_to_all | solution.py:78
  674.4 18.1 %reshape.48 = f32[256,5,2,16,32]{4,3,2,1,0:T(8,128)} reshape(f32[16,81920]{1,0:T(8,128)} %reduce) | data formatting | bytes 10485760
  692.5 18.5 %copy.44 = f32[5,2,32,16,16,16]{2,5,4,3,1,0:T(8,128)S(1)} copy(f32[5,2,32,16,16,16]{2,4,1,0,5,3:T(8,128)} %bitcast.123) | data formatting | bytes 10485760 | tf_op jit(solution)/shard_map/all_to_all | solution.py:78
  711.0 7.5 fusion.79
  718.6 8.6 %copy.53 = f32[5,1,32,256,16]{3,4,2,0,1:T(8,128)S(1)} copy(f32[5,1,32,256,16]{2,4,3,1,0:T(8,128)} %get-tuple-element.139) | data formatting | bytes 5242880
  727.2 4.8 fusion.35
  732.0 4.7 fusion.33
  736.6 8.7 %copy.52 = f32[5,1,32,256,16]{3,4,2,0,1:T(8,128)S(1)} copy(f32[5,1,32,256,16]{2,4,3,1,0:T(8,128)} %get-tuple-element.138) | data formatting | bytes 5242880
  745.3 5.1 subtract_bitcast_fusion
  750.4 3.3 add_bitcast_fusion
  754.5 2.9 copy.47
  (28 shorter events, 8.2 us)
Async XLA Ops:
  0.0 485.7 %copy-start = (f32[5,16]{1,0:T(8,128)S(1)}, f32[5,16]{1,0:T(8,128)}, u32[]{:S(2)}) copy-start(f32[5,16]{1,0:T(8,128)} %param.15) | copy-start | bytes 964
  1.5 7.2 copy-start.3
  8.7 11.3 %copy-start.5 = (s32[4]{0:T(128)S(1)}, s32[4]{0:T(128)}, u32[]{:S(2)}) copy-start(s32[4]{0:T(128)} %param.13) | copy-start | bytes 52
  13.5 16.3 %collective-permute-start = (bf16[16,2,32,1,256]{4,2,3,1,0:T(8,128)(2,1)S(1)}, bf16[16,2,32,1,256]{4,2,3,1,0:T(8,128)(2,1)S(1)}, u32[]{:S(2)}, u32[]{:S(2)}) collective-permute-start(bf16[16,2,32,1,256]{4,2,3,1,0:T(8,128)(2,1)S(1)} %copy.37), channel_id=1, source_target_pairs={{0,1},{1,2},{2,3},{3,4},{4,5},{5,6},{6,7},{7,8},{8,9},{9,10},{10,1... | collective-permute-start | bytes 1572872 | tf_op jit(solution)/shard_map/ppermute | solution.py:14
  18.1 12.6 %collective-permute-start.1 = (bf16[16,2,32,1,256]{4,2,3,1,0:T(8,128)(2,1)S(1)}, bf16[16,2,32,1,256]{4,2,3,1,0:T(8,128)(2,1)S(1)}, u32[]{:S(2)}, u32[]{:S(2)}) collective-permute-start(bf16[16,2,32,1,256]{4,2,3,1,0:T(8,128)(2,1)S(1)} %copy.38), channel_id=1, source_target_pairs={{1,0},{2,1},{3,2},{4,3},{5,4},{6,5},{7,6},{8,7},{9,8},{10,9},{11,1... | collective-permute-start | bytes 1572872 | tf_op jit(solution)/shard_map/ppermute | solution.py:17
  31.8 13.6 %copy-start.2 = (bf16[2,768,64]{1,2,0:T(8,128)(2,1)S(1)}, bf16[2,768,64]{1,2,0:T(8,128)(2,1)}, u32[]{:S(2)}) copy-start(bf16[2,768,64]{1,2,0:T(8,128)(2,1)} %param.11) | copy-start | bytes 589828
  468.6 11.0 %copy-start.4 = (pred[16,16]{1,0:T(8,128)(4,1)S(1)}, pred[16,16]{1,0:T(8,128)(4,1)}, u32[]{:S(2)}) copy-start(pred[16,16]{1,0:T(8,128)(4,1)} %copy-done.3) | copy-start | bytes 772
  745.3 5.1 copy-start.1
where the time goes:
time: 767 us; the launch traced here: 758 us
  local copies, waits for them, and re-layouts  289 us (38%)
  other arithmetic  228 us (30%)
  blocking collectives  121 us (16%)
  matrix products  94.5 us (12%)
  loops' own time  8.59 us (1%)
    reshape x4, local copies, waits for them, and re-layouts, estimate_block(): jnp.stack(ky_layers, axis=2).reshape(frame_block, -1, row_count * kx_count)  151 us
    all_to_all x1, blocking collectives, on_device(): lax.all_to_all(coefficients, 'ky', split_axis=4, concat_axis=3, tiled=True)  121 us
    another operation x12, other arithmetic, estimate_block(): jnp.stack([jnp.roll(ky_slice, -offsets[kx_tap], axis=4) for kx_tap in ran...  114 us
    another operation x12, other arithmetic, estimate_block(): jnp.stack(ky_layers, axis=2).reshape(frame_block, -1, row_count * kx_count)  68.6 us
    unnamed x17, local copies, waits for them, and re-layouts  64.4 us
    dot_general x4, matrix products, estimate_block(): jnp.einsum('io,fir->for', weights, sources, preferred_element_type=jnp.fl...  58.8 us
    all_to_all x2, local copies, waits for them, and re-layouts, on_device(): lax.all_to_all(coefficients, 'ky', split_axis=4, concat_axis=3, tiled=True)  19 us
    dot_general x1, matrix products, on_device(): jnp.einsum('bf,fpcrx->bpcrx', temporal_basis, filled, precision=high)  17.8 us
  transfers between devices with their start and end apart: 2, of which 1 were waited for; matrix products, arithmetic and copies ran while one was open for 0% of the time, Pallas kernels for 0%

commit v1 on v0

--- a/solution.py
+++ b/solution.py
@@ -1,9 +1,22 @@
+import functools
+
 import jax
 import jax.numpy as jnp
+import ml_dtypes
+import numpy as np
 from jax import lax
+from jax.experimental import pallas as pl
+from jax.experimental.pallas import tpu as pltpu
 from jax.sharding import PartitionSpec as P
 
 frame_block = 4
+batch = 4
+together = 2
+pair = 2
+sample_bound = 6.0
+half_top = 60000.0
+lanes = 128
+sublanes = 8
 
 
 def padded_2(block, sides, width):
@@ -39,7 +52,7 @@
     return jnp.stack([out_real, out_imag], axis=1) * scale
 
 
-def on_device(kspace, kernel, pattern, offsets, segment, temporal_basis):
+def plain_device(kspace, kernel, pattern, offsets, segment, temporal_basis):
     frame_total, _, coil_count, row_count, kx_count = kspace.shape
     group_count = kernel.shape[0]
     group_frames = frame_total // group_count
@@ -79,6 +92,416 @@
     return inverse_rows(swapped)
 
 
+class Filler:
+
+    def __init__(self, refs, scratch, parts, kx_count):
+        self.place, self.pattern, self.segment, self.offset, self.basis, self.kernel = refs
+        self.source, self.product, self.totals, self.taps, self.order, self.count, self.scale = (
+            scratch
+        )
+        self.parts = parts
+        self.kx_count = kx_count
+        self.frame_total = self.pattern.shape[0]
+        self.row_total = self.segment.shape[0]
+        self.basis_count = self.basis.shape[0]
+        self.group_count = self.kernel.shape[0]
+        self.group_frames = self.frame_total // self.group_count
+        self.tap_count = self.offset.shape[0]
+        self.coil_count = parts // 2
+
+    def row_of(self, local):
+        row = self.place[0] + local
+        inside = (row >= 0) & (row < self.row_total)
+        return self.segment[jnp.clip(row, 0, self.row_total - 1)], inside
+
+    def prepare(self, shape):
+        self.totals[...] = jnp.zeros_like(self.totals)
+        width = self.tap_count * self.coil_count
+        strength = jnp.float32(1.0)
+        for group in range(self.group_count):
+            for tap in range(3):
+                joined = jnp.concatenate(
+                    [
+                        self.kernel[group, :, (p * 3 + tap) * width : (p * 3 + tap + 1) * width]
+                        for p in range(2)
+                    ],
+                    axis=1,
+                )
+                self.taps[group, tap * self.parts : (tap + 1) * self.parts, :] = joined
+            reach = jnp.sum(jnp.abs(self.kernel[group].astype(jnp.float32)), axis=1, keepdims=True)
+            strength = jnp.maximum(strength, jnp.max(reach))
+        extent = jnp.float32(0.0)
+        for v in range(self.basis_count):
+            extent_v = jnp.float32(0.0)
+            for frame in range(self.frame_total):
+                extent_v = extent_v + jnp.abs(self.basis[v, frame])
+            extent = jnp.maximum(extent, extent_v)
+        bound = jnp.maximum(sample_bound * extent * strength, 1e-30)
+        scale = half_top / jnp.full(shape, bound, jnp.float32)
+        self.scale[0] = jnp.max(scale)
+        return 1.0 / scale
+
+    def listing(self, slot, local):
+        value, inside = self.row_of(local)
+        filled = jnp.int32(0)
+        doubled = jnp.int32(0)
+        again, _ = self.row_of(local)
+        for frame in range(self.frame_total):
+            taken = (value == self.pattern[frame]) & inside
+            self.order[slot * self.frame_total + filled] = frame
+            filled = filled + taken.astype(jnp.int32)
+            doubled = doubled + (taken & (again != self.pattern[frame])).astype(jnp.int32)
+        self.count[2 * slot] = filled
+        self.count[2 * slot + 1] = doubled
+
+    def shifted(self, entry):
+        narrow = self.source[entry].astype(jnp.bfloat16)
+        shifts = [
+            lax.rem(self.kx_count - self.offset[tap], self.kx_count)
+            for tap in range(self.tap_count)
+        ]
+        return jnp.concatenate(
+            [
+                pltpu.roll(narrow[p * self.coil_count : (p + 1) * self.coil_count], shift, axis=1)
+                for p in range(2)
+                for shift in shifts
+            ],
+            axis=0,
+        )
+
+    def add(self, target, weights, entries):
+        for start in range(0, self.parts, sublanes):
+            pieces = [
+                ref[entry, offset + start : offset + start + sublanes, :]
+                for ref, entry, offset in entries
+            ]
+            for v in range(self.basis_count):
+                total = self.totals[target, v, start : start + sublanes, :]
+                for weight, piece in zip(weights, pieces):
+                    total = total + weight[v] * piece
+                self.totals[target, v, start : start + sublanes, :] = total
+
+    def multiply(self, entry, group, tap, offset):
+        self.product[entry, offset : offset + self.parts] = jnp.dot(
+            self.taps[group, tap * self.parts : (tap + 1) * self.parts],
+            self.shifted(entry),
+            preferred_element_type=jnp.float32,
+        )
+
+    def row(self, slot, local, fetch, targets):
+        listed = self.count[2 * slot]
+        parts = self.parts
+        neighbours = [self.row_of(local + 1 - tap) for tap in range(3)]
+
+        def load(entry, position):
+            frame = self.order[slot * self.frame_total + jnp.minimum(position, listed - 1)]
+            fetch(entry, frame)
+            scale = jnp.where(position < listed, self.scale[0], 0.0)
+            direct = [self.basis[v, frame] * scale for v in range(self.basis_count)]
+            wanted = self.pattern[frame]
+            masked = [
+                [jnp.where(inside & (value != wanted), weight, 0.0) for weight in direct]
+                for value, inside in neighbours
+            ]
+            return frame // self.group_frames, direct, masked
+
+        def batch_at(base, size):
+            each = range(size)
+            loaded = [load(e, base + e) for e in each]
+            sides = [tap for tap in (0, 2) if targets[tap] is not None]
+            for e in each:
+                for tap in sides:
+                    self.multiply(e, loaded[e][0], tap, tap // 2 * parts)
+            if targets[1] is not None:
+                self.add(
+                    targets[1], [loaded[e][1] for e in each], [(self.source, e, 0) for e in each]
+                )
+            for tap in sides:
+                self.add(
+                    targets[tap],
+                    [loaded[e][2][tap] for e in each],
+                    [(self.product, e, tap // 2 * parts) for e in each],
+                )
+
+        def full(index, carry):
+            batch_at(index * batch, batch)
+            return carry
+
+        whole = listed // batch
+        rest = listed - whole * batch
+        large = (rest > batch // 2).astype(jnp.int32)
+        lax.fori_loop(0, whole + large, full, 0)
+
+        @pl.when((rest > 0) & (large == 0))
+        def _():
+            batch_at(whole * batch, batch // 2)
+
+        def centre(index, carry):
+            group, _, masked = load(0, index)
+            self.multiply(0, group, 1, 0)
+            self.add(targets[1], [masked[1]], [(self.product, 0, 0)])
+            return carry
+
+        if targets[1] is not None:
+            lax.fori_loop(0, jnp.where(self.count[2 * slot + 1] > 0, listed, 0), centre, 0)
+
+
+def fill_kernel(
+    row_count,
+    place_ref,
+    pattern_ref,
+    segment_ref,
+    offset_ref,
+    basis_ref,
+    block_ref,
+    kernel_ref,
+    out_ref,
+    inverse_ref,
+    samples,
+    *scratch,
+):
+    _, halves, _, _ = samples.shape
+    together, parts, _, kx_count = block_ref.shape
+    refs = (place_ref, pattern_ref, segment_ref, offset_ref, basis_ref, kernel_ref)
+    filler = Filler(refs, scratch, parts, kx_count)
+    step = pl.program_id(0)
+
+    for t in range(together):
+        values = block_ref[t].astype(jnp.float32).reshape(parts * row_count, kx_count)
+        for half in range(halves):
+            samples[step * together + t, half] = values[:, half * lanes : (half + 1) * lanes]
+
+    @pl.when(step == 0)
+    def _():
+        inverse_ref[...] = filler.prepare(inverse_ref.shape)
+
+        def listing(row, carry):
+            filler.listing(row, row)
+            return carry
+
+        lax.fori_loop(0, row_count, listing, 0)
+
+    def rows(row, carry):
+        def fetch(entry, frame):
+            for half in range(halves):
+                filler.source[entry, :, half * lanes : (half + 1) * lanes] = samples[
+                    frame, half, pl.ds(row, parts, stride=row_count), :
+                ]
+
+        filler.row(row, row, fetch, (row + 2, row + 1, row))
+        return carry
+
+    def pack(index, carry):
+        devices, basis_count, stored, _ = out_ref.shape
+        pitch = row_count // pair
+        columns = stored // pitch
+        for v in range(basis_count):
+            turned = jnp.concatenate(
+                [filler.totals[pair * index + 1 + j, v] for j in range(pair)], axis=0
+            ).T
+            for d in range(devices):
+                out_ref[d, v, pl.ds(index, columns, stride=pitch), :] = turned[
+                    d * columns : (d + 1) * columns
+                ]
+        return carry
+
+    @pl.when(step == pl.num_programs(0) - 1)
+    def _():
+        lax.fori_loop(0, row_count, rows, 0)
+        lax.fori_loop(0, row_count // pair, pack, 0)
+
+
+def edge_kernel(
+    row_count,
+    place_ref,
+    pattern_ref,
+    segment_ref,
+    offset_ref,
+    basis_ref,
+    low_ref,
+    high_ref,
+    kernel_ref,
+    out_ref,
+    *scratch,
+):
+    _, parts, kx_count = low_ref.shape
+    refs = (place_ref, pattern_ref, segment_ref, offset_ref, basis_ref, kernel_ref)
+    filler = Filler(refs, scratch, parts, kx_count)
+    filler.prepare((sublanes, lanes))
+    sides = ((-1, low_ref, (0, None, None)), (row_count, high_ref, (None, None, 1)))
+    for slot, (local, ref, targets) in enumerate(sides):
+        filler.listing(slot, local)
+
+        def fetch(entry, frame):
+            filler.source[entry] = ref[frame].astype(jnp.float32)
+
+        filler.row(slot, local, fetch, targets)
+    devices, basis_count, columns, _ = out_ref.shape
+    for v in range(basis_count):
+        turned = jnp.concatenate([filler.totals[0, v], filler.totals[1, v]], axis=0).T
+        for d in range(devices):
+            out_ref[d, v] = turned[d * columns : (d + 1) * columns]
+
+
+def image_kernel(row_count, coil_count, inverse_ref, block_ref, table_ref, out_ref, held):
+    devices, _, stored, _ = block_ref.shape
+    pair, part_count, length, width = held.shape
+    pitch = row_count // pair
+    columns = stored // pitch
+    parts = part_count * coil_count
+    row_total = devices * row_count
+    scale = inverse_ref[0:1, 0:1]
+    for x in range(columns):
+        turned = block_ref[:, 0, x * pitch : (x + 1) * pitch, :].reshape(width, lanes).T
+        for j in range(pair):
+            for p in range(part_count):
+                start = j * parts + p * coil_count
+                held[j, p, pl.ds(x, coil_count, stride=columns), :] = turned[
+                    start : start + coil_count
+                ]
+    for start in range(0, length, lanes):
+        left = jnp.concatenate(
+            [
+                held[j, p, start : start + lanes, :]
+                for p in range(part_count)
+                for j in range(pair)
+            ],
+            axis=1,
+        )
+        coarse = left.astype(jnp.bfloat16)
+        fine = (left - coarse.astype(jnp.float32)).astype(jnp.bfloat16)
+        result = jnp.dot(coarse, table_ref[0], preferred_element_type=jnp.float32)
+        result = result + jnp.dot(coarse, table_ref[1], preferred_element_type=jnp.float32)
+        result = result + jnp.dot(fine, table_ref[0], preferred_element_type=jnp.float32)
+        result = result * scale
+        for p in range(part_count):
+            out_ref[0, p, start : start + lanes, :] = result[:, p * row_total : (p + 1) * row_total]
+
+
+def inverse_table(row_total, pair):
+    row = np.arange(row_total).reshape(-1, pair).T.reshape(-1)
+    index = np.arange(row_total)
+    angle = (row[:, None] * index[None, :] % row_total) * (2.0 * np.pi / row_total)
+    cosine = np.cos(angle) / np.sqrt(row_total)
+    sine = np.sin(angle) / np.sqrt(row_total)
+    full = np.block([[cosine, sine], [-sine, cosine]]).astype(np.float32)
+    coarse = full.astype(ml_dtypes.bfloat16)
+    fine = (full - coarse.astype(np.float32)).astype(ml_dtypes.bfloat16)
+    return np.stack([coarse, fine])
+
+
+def on_device(kspace, kernel, pattern, offsets, segment, temporal_basis):
+    frame_total, part_count, coil_count, row_count, kx_count = kspace.shape
+    devices = lax.axis_size("ky")
+    columns = kx_count // devices
+    parts = part_count * coil_count
+    row_total = row_count * devices
+    tap_count = offsets.shape[0]
+    fits = (
+        2 * parts == lanes
+        and row_count == 2 * sublanes
+        and columns % sublanes == 0
+        and row_total == 2 * lanes
+        and kx_count % lanes == 0
+        and tap_count * coil_count == lanes
+        and frame_total % together == 0
+    )
+    if not fits:
+        return plain_device(kspace, kernel, pattern, offsets, segment, temporal_basis)
+
+    basis_count = temporal_basis.shape[0]
+    group_count = kernel.shape[0]
+    stored = columns * row_count // pair
+    halves = kx_count // lanes
+
+    forward = [(i, i + 1) for i in range(devices - 1)]
+    backward = [(i + 1, i) for i in range(devices - 1)]
+    edge_shape = (frame_total, parts, kx_count)
+    low = lax.ppermute(kspace[:, :, :, -1, :].reshape(edge_shape), "ky", forward)
+    high = lax.ppermute(kspace[:, :, :, 0, :].reshape(edge_shape), "ky", backward)
+
+    place = (lax.axis_index("ky") * row_count).astype(jnp.int32).reshape(1)
+    kernel_rows = kernel.transpose(0, 2, 1)
+    fill_work = 4 * frame_total * row_count * kx_count * kernel.shape[1] * parts
+
+    scalar = pl.BlockSpec(memory_space=pltpu.SMEM)
+
+    def scratch(rows, slots):
+        return [
+            pltpu.VMEM((batch, parts, kx_count), jnp.float32),
+            pltpu.VMEM((batch, 2 * parts, kx_count), jnp.float32),
+            pltpu.VMEM((rows, basis_count, parts, kx_count), jnp.float32),
+            pltpu.VMEM((group_count, 3 * parts, tap_count * parts), jnp.bfloat16),
+            pltpu.SMEM((slots * frame_total + 1,), jnp.int32),
+            pltpu.SMEM((2 * slots,), jnp.int32),
+            pltpu.SMEM((1,), jnp.float32),
+        ]
+
+    scalars = (place, pattern, segment, offsets, temporal_basis)
+    payload, inverse = pl.pallas_call(
+        functools.partial(fill_kernel, row_count),
+        grid=(frame_total // together,),
+        in_specs=[scalar] * len(scalars)
+        + [
+            pl.BlockSpec((together, parts, row_count, kx_count), lambda t: (t, 0, 0, 0)),
+            pl.BlockSpec(kernel_rows.shape, lambda t: (0, 0, 0)),
+        ],
+        out_specs=[
+            pl.BlockSpec((devices, basis_count, stored, lanes), lambda t: (0, 0, 0, 0)),
+            pl.BlockSpec((sublanes, lanes), lambda t: (0, 0)),
+        ],
+        out_shape=[
+            jax.ShapeDtypeStruct((devices, basis_count, stored, lanes), jnp.float32),
+            jax.ShapeDtypeStruct((sublanes, lanes), jnp.float32),
+        ],
+        scratch_shapes=[
+            pltpu.VMEM((frame_total, halves, parts * row_count, lanes), jnp.float32)
+        ]
+        + scratch(row_count + 2, row_count),
+        cost_estimate=pl.CostEstimate(flops=fill_work, bytes_accessed=0, transcendentals=0),
+        name="fill",
+    )(*scalars, kspace.reshape(frame_total, parts, row_count, kx_count), kernel_rows)
+    whole = pl.BlockSpec(memory_space=pltpu.VMEM)
+    edges = pl.pallas_call(
+        functools.partial(edge_kernel, row_count),
+        in_specs=[scalar] * len(scalars) + [whole] * 3,
+        out_specs=whole,
+        out_shape=jax.ShapeDtypeStruct((devices, basis_count, columns, lanes), jnp.float32),
+        scratch_shapes=scratch(2, 2),
+        name="edge",
+    )(*scalars, low, high, kernel_rows)
+    spread = payload.reshape(devices, basis_count, columns, row_count // pair, lanes)
+    place_in = lax.broadcasted_iota(jnp.int32, spread.shape, 3)
+    lane = lax.broadcasted_iota(jnp.int32, spread.shape, 4)
+    outer = jnp.where(lane < parts, 0, row_count // pair - 1) == place_in
+    spread = spread + jnp.where(outer, edges[:, :, :, None, :], 0.0)
+    payload = spread.astype(jnp.float16).reshape(devices, basis_count, stored, lanes)
+    swapped = lax.all_to_all(
+        payload, "ky", split_axis=0, concat_axis=0, tiled=True
+    ).astype(jnp.float32)
+
+    table = jnp.asarray(inverse_table(row_total, pair))
+    length = coil_count * columns
+    images = pl.pallas_call(
+        functools.partial(image_kernel, row_count, coil_count),
+        grid=(basis_count,),
+        in_specs=[
+            pl.BlockSpec((sublanes, lanes), lambda v: (0, 0)),
+            pl.BlockSpec((devices, 1, stored, lanes), lambda v: (0, v, 0, 0)),
+            pl.BlockSpec(table.shape, lambda v: (0, 0, 0)),
+        ],
+        out_specs=pl.BlockSpec((1, part_count, length, row_total), lambda v: (v, 0, 0, 0)),
+        out_shape=jax.ShapeDtypeStruct(
+            (basis_count, part_count, length, row_total), jnp.float32
+        ),
+        scratch_shapes=[
+            pltpu.VMEM((pair, part_count, length, row_total // pair), jnp.float32)
+        ],
+        name="image",
+    )(inverse, swapped, table)
+    return images.reshape(basis_count, part_count, coil_count, columns, row_total)
+
+
 def solution(mesh):
     return jax.shard_map(
         on_device,

time: 767 us -> 128 us (0.17); the launches traced: 758 us -> 127 us
  local copies, waits for them, and re-layouts: 289 us -> 6.5 us
  other arithmetic: 228 us -> 6.48 us
  matrix products: 94.5 us -> 0 us
  blocking collectives: 121 us -> 66.4 us
  Pallas kernels: 0 us -> 41.6 us
  loops' own time: 8.59 us -> 0 us
    another operation x24 -> x0, other arithmetic: 183 us -> none  [the longest x12 114 us: estimate_block(): jnp.stack([jnp.roll(ky_slice, -offsets[kx_tap], axis=4) for kx_tap in ran...]
    reshape x4 -> x0, local copies, waits for them, and re-layouts: 151 us -> none  [estimate_block(): jnp.stack(ky_layers, axis=2).reshape(frame_block, -1, row_count * kx_count)]
    dot_general x9 -> x0, matrix products: 94.5 us -> none  [the longest x4 58.8 us: estimate_block(): jnp.einsum('io,fir->for', weights, sources, preferred_element_type=jnp.fl...]
    unnamed x17 -> x6, local copies, waits for them, and re-layouts: 64.4 us -> 1.85 us
    all_to_all x1, blocking collectives: 121 us -> 66.4 us  [on_device(): lax.all_to_all(payload, 'ky', split_axis=0, concat_axis=0, tiled=True)]
    pallas_call x0 -> x3, Pallas kernels: none -> 41.6 us  [the longest x1 27.8 us: on_device(): pl.pallas_call(functools.partial(fill_kernel, row_count), grid=(frame_tot...]
    slice x9 -> x1, local copies, waits for them, and re-layouts: 24.3 us -> 4.56 us  [on_device(): kspace[:, :, :, 0, :].reshape(edge_shape)]
    all_to_all x2 -> x0, local copies, waits for them, and re-layouts: 19 us -> none  [on_device(): lax.all_to_all(coefficients, 'ky', split_axis=4, concat_axis=3, tiled=True)]
  transfers between devices with their start and end apart: 2 -> 2, of which waited for: 1 -> 0; matrix products, arithmetic and copies ran while one was open for 0% -> 0% of each run, Pallas kernels for 0% -> 22%
where the time goes in v1:
time: 128 us; the launch traced here: 127 us
  blocking collectives  66.4 us (52%)
  Pallas kernels  41.6 us (32%)
  local copies, waits for them, and re-layouts  6.5 us (5%)
  other arithmetic  6.48 us (5%)
  starting transfers between devices  6.45 us (5%)
    all_to_all x1, blocking collectives, on_device(): lax.all_to_all(payload, 'ky', split_axis=0, concat_axis=0, tiled=True)  66.4 us
    pallas_call x1, Pallas kernels, on_device(): pl.pallas_call(functools.partial(fill_kernel, row_count), grid=(frame_tot...  27.8 us
    pallas_call x1, Pallas kernels, on_device(): pl.pallas_call(functools.partial(image_kernel, row_count, coil_count), gr...  10 us
    slice x1, local copies, waits for them, and re-layouts, on_device(): kspace[:, :, :, 0, :].reshape(edge_shape)  4.56 us
    ppermute x1, starting transfers between devices, on_device(): lax.ppermute(kspace[:, :, :, -1, :].reshape(edge_shape), 'ky', forward)  4.53 us
    pallas_call x1, Pallas kernels, on_device(): pl.pallas_call(functools.partial(edge_kernel, row_count), in_specs=[scala...  3.8 us
    convert_element_type x1, other arithmetic, on_device(): spread.astype(jnp.float16).reshape(devices, basis_count, stored, lanes)  3.66 us
    convert_element_type x1, other arithmetic, on_device(): swapped = lax.all_to_all(payload, 'ky', split_axis=0, concat_axis=0, tile...  2.82 us
  transfers between devices with their start and end apart: 2, of which 0 were waited for; matrix products, arithmetic and copies ran while one was open for 0% of the time, Pallas kernels for 22%

profile of v1, /device:TPU:1, one launch (start us, length us, event | category | flops | bytes accessed | tf_op | source)
XLA Modules:
  0.0 127.5 jit_solution(11395011883530603132)
XLA Ops:
  0.0 4.6 %fusion.2 = (bf16[16,2,32,1,256]{4,3,2,1,0:T(2,128)(2,1)S(1)}, bf16[16,2,32,1,256]{4,3,2,1,0:T(2,128)(2,1)S(1)}) fusion(bf16[16,2,32,16,256]{4,3,2,1,0:T(8,128)(2,1)} %param.7), kind=kLoop, calls=%fused_computation.4 | loop fusion | bytes 2097152 | tf_op jit(solution)/shard_map/slice | solution.py:421
  4.6 0.1 copy.10
  4.7 4.5 %collective-permute-start = (bf16[16,64,256]{2,1,0:T(8,128)(2,1)S(1)}, bf16[16,64,256]{2,1,0:T(8,128)(2,1)S(1)}, u32[]{:S(2)}, u32[]{:S(2)}) collective-permute-start(bf16[16,64,256]{2,1,0:T(8,128)(2,1)S(1)} %bitcast.12), channel_id=1, source_target_pairs={{0,1},{1,2},{2,3},{3,4},{4,5},{5,6},{6,7},{7,8},{8,9},{9,10},{10,1... | collective-permute-start | bytes 1572872 | tf_op jit(solution)/shard_map/ppermute | solution.py:420
  9.2 0.1 copy.11
  9.4 1.9 %collective-permute-start.1 = (bf16[16,64,256]{2,1,0:T(8,128)(2,1)S(1)}, bf16[16,64,256]{2,1,0:T(8,128)(2,1)S(1)}, u32[]{:S(2)}, u32[]{:S(2)}) collective-permute-start(bf16[16,64,256]{2,1,0:T(8,128)(2,1)S(1)} %bitcast.13), channel_id=1, source_target_pairs={{1,0},{2,1},{3,2},{4,3},{5,4},{6,5},{7,6},{8,7},{9,8},{10,9},{11,1... | collective-permute-start | bytes 1572872 | tf_op jit(solution)/shard_map/ppermute | solution.py:421
  11.3 27.8 %fill.1 = (f32[16,5,128,128]{3,2,1,0:T(8,128)}, f32[8,128]{1,0:T(8,128)}) custom-call(s32[1]{0:T(128)} %bitcast.place_ref, s32[16]{0:T(128)} %pattern_ref.3, s32[256]{0:T(256)} %segment_ref.3, s32[4]{0:T(128)} %offset_ref.3, f32[5,16]{1,0:T(8,128)} %basis_ref.3, bf16[16,64,16,256]{3,2,1,0:T(8,128)(2,1)} %bitcast.14, bf16[2,64,768]{2,1,0:T(8,128)(2,1)} %bitcast.15), custom_call_target="tpu_custom_call" | custom-call | flops 12884901888 | tf_op jit(solution)/shard_map/fill/pallas_call | solution.py:441
  39.1 0.1 iota.20
  39.2 0.0 collective-permute-done.low_ref
  39.2 0.0 copy-start
  39.2 0.0 collective-permute-done.1.high_ref
  39.2 0.8 copy-done
  40.0 0.0 copy-start.1
  40.0 0.8 copy-done.1
  40.8 3.8 %edge.1 = f32[16,5,16,128]{3,2,1,0:T(8,128)} custom-call(s32[1]{0:T(128)} %bitcast.place_ref, s32[16]{0:T(128)} %pattern_ref.3, s32[256]{0:T(256)} %segment_ref.3, s32[4]{0:T(128)} %offset_ref.3, f32[5,16]{1,0:T(8,128)} %basis_ref.3, bf16[16,64,256]{2,1,0:T(8,128)(2,1)} %copy-done, bf16[16,64,256]{2,1,0:T(8,128)(2,1)} %copy-done.1, bf16[2,64,768]{2,1,0:T(8,128)(2,1)} %bitcast.16), custom_call_target="tpu_custom_call" | custom-call | tf_op jit(solution)/shard_map/edge/pallas_call | solution.py:465
  44.6 3.7 %fusion.1 = f16[16,5,128,128]{3,2,1,0:T(8,128)(2,1)S(1)} fusion(f32[16,5,128,128]{3,2,1,0:T(8,128)} %get-tuple-element.8, f32[16,5,16,128]{3,2,1,0:T(8,128)} %edge.1, s32[128]{0:T(128)S(1)} %compare_select_fusion, s32[128]{0:T(128)S(1)} %iota.20), kind=kLoop, calls=%fused_computation.2 | loop fusion | flops 5242880 | bytes 8520704 | tf_op jit(solution)/shard_map/convert_element_type | solution.py:478
  48.3 66.4 %all_to_all.5 = f16[16,5,128,128]{3,2,1,0:T(8,128)(2,1)S(1)} all-to-all(f16[16,5,128,128]{3,2,1,0:T(8,128)(2,1)S(1)} %fusion.1), channel_id=1, replica_groups=mesh['study'=2,'ky'=16] {'ky'}, dimensions={0} | all-to-all | bytes 5242880 | tf_op jit(solution)/shard_map/all_to_all | solution.py:479
  114.6 2.8 %convert_element_type.8.block_ref = f32[16,5,128,128]{3,2,1,0:T(8,128)} convert(f16[16,5,128,128]{3,2,1,0:T(8,128)(2,1)S(1)} %all_to_all.5) | non-fusion elementwise | flops 1310720 | bytes 7864320 | tf_op jit(solution)/shard_map/convert_element_type | solution.py:481
  117.4 10.0 %image.1 = f32[5,2,512,256]{3,2,1,0:T(8,128)} custom-call(f32[8,128]{1,0:T(8,128)} %get-tuple-element.7.inverse_ref, f32[16,5,128,128]{3,2,1,0:T(8,128)} %convert_element_type.8.block_ref, bf16[2,512,512]{2,1,0:T(8,128)(2,1)} %constant.16.clone.table_ref), custom_call_target="tpu_custom_call" | custom-call | tf_op jit(solution)/shard_map/image/pallas_call | solution.py:485
  (2 shorter events, 0.0 us)
Async XLA Ops:
  4.7 34.5 %collective-permute-start = (bf16[16,64,256]{2,1,0:T(8,128)(2,1)S(1)}, bf16[16,64,256]{2,1,0:T(8,128)(2,1)S(1)}, u32[]{:S(2)}, u32[]{:S(2)}) collective-permute-start(bf16[16,64,256]{2,1,0:T(8,128)(2,1)S(1)} %bitcast.12), channel_id=1, source_target_pairs={{0,1},{1,2},{2,3},{3,4},{4,5},{5,6},{6,7},{7,8},{8,9},{9,10},{10,1... | collective-permute-start | bytes 1572872 | tf_op jit(solution)/shard_map/ppermute | solution.py:420
  9.4 29.8 %collective-permute-start.1 = (bf16[16,64,256]{2,1,0:T(8,128)(2,1)S(1)}, bf16[16,64,256]{2,1,0:T(8,128)(2,1)S(1)}, u32[]{:S(2)}, u32[]{:S(2)}) collective-permute-start(bf16[16,64,256]{2,1,0:T(8,128)(2,1)S(1)} %bitcast.13), channel_id=1, source_target_pairs={{1,0},{2,1},{3,2},{4,3},{5,4},{6,5},{7,6},{8,7},{9,8},{10,9},{11,1... | collective-permute-start | bytes 1572872 | tf_op jit(solution)/shard_map/ppermute | solution.py:421
  39.2 0.8 copy-start
  40.0 0.8 copy-start.1

commit v2 on v1

--- a/solution.py
+++ b/solution.py
@@ -9,10 +9,10 @@
 from jax.experimental.pallas import tpu as pltpu
 from jax.sharding import PartitionSpec as P
 
+
 frame_block = 4
 batch = 4
-together = 2
-pair = 2
+together = 8
 sample_bound = 6.0
 half_top = 60000.0
 lanes = 128
@@ -246,7 +246,65 @@
             lax.fori_loop(0, jnp.where(self.count[2 * slot + 1] > 0, listed, 0), centre, 0)
 
 
-def fill_kernel(
+def convert_frames(block_ref, samples):
+    together, parts, row_count, kx_count = block_ref.shape
+    for t in range(together):
+        values = block_ref[t].astype(jnp.float32).reshape(parts * row_count, kx_count)
+        for half in range(kx_count // lanes):
+            samples[pl.program_id(0) * together + t, half] = values[
+                :, half * lanes : (half + 1) * lanes
+            ]
+
+
+def list_rows(filler, row_count):
+    def listing(row, carry):
+        filler.listing(row, row)
+        return carry
+
+    lax.fori_loop(0, row_count, listing, 0)
+
+
+def add_row(filler, samples, row_count, row):
+    halves = samples.shape[1]
+
+    def fetch(entry, frame):
+        for half in range(halves):
+            filler.source[entry, :, half * lanes : (half + 1) * lanes] = samples[
+                frame, half, pl.ds(row, filler.parts, stride=row_count), :
+            ]
+
+    filler.row(row, row, fetch, (row + 2, row + 1, row))
+
+
+def pack_rows(filler, own, out_ref, row_at):
+    devices, basis_count, stored, _ = out_ref.shape
+    held = stored // sublanes
+
+    def pack(index, carry):
+        row = row_at(index)
+        for v in range(basis_count):
+            turned = jnp.concatenate(
+                [filler.totals[row + 1, v], filler.totals[row + 2, v]], axis=0
+            ).T
+            rolled = pltpu.roll(turned, lanes // 2, axis=1)
+            turned = turned.reshape(devices, 2, sublanes, lanes)
+            rolled = rolled.reshape(devices, 2, sublanes, lanes)
+            lower = lax.broadcasted_iota(jnp.int32, (sublanes, lanes), 1) < lanes // 2
+            for d in range(devices):
+                apart = d ^ own
+                slot = (apart & 1) * (devices // 2) + (apart >> 1)
+                out_ref[slot, v, pl.ds(2 * index, sublanes, stride=held), :] = jnp.where(
+                    lower, turned[d, 0], rolled[d, 1]
+                )
+                out_ref[slot, v, pl.ds(2 * index + 1, sublanes, stride=held), :] = jnp.where(
+                    lower, rolled[d, 0], turned[d, 1]
+                )
+        return carry
+
+    lax.fori_loop(0, held // 2, pack, 0)
+
+
+def inner_kernel(
     row_count,
     place_ref,
     pattern_ref,
@@ -257,115 +315,128 @@
     kernel_ref,
     out_ref,
     inverse_ref,
+    rest_ref,
+    first_ref,
+    last_ref,
     samples,
     *scratch,
 ):
-    _, halves, _, _ = samples.shape
-    together, parts, _, kx_count = block_ref.shape
+    frame_total, halves, _, _ = samples.shape
+    _, parts, _, kx_count = block_ref.shape
     refs = (place_ref, pattern_ref, segment_ref, offset_ref, basis_ref, kernel_ref)
     filler = Filler(refs, scratch, parts, kx_count)
-    step = pl.program_id(0)
-
-    for t in range(together):
-        values = block_ref[t].astype(jnp.float32).reshape(parts * row_count, kx_count)
-        for half in range(halves):
-            samples[step * together + t, half] = values[:, half * lanes : (half + 1) * lanes]
-
-    @pl.when(step == 0)
+    quarter = row_count // 4
+    convert_frames(block_ref, samples)
+
+    @pl.when(pl.program_id(0) == 0)
     def _():
         inverse_ref[...] = filler.prepare(inverse_ref.shape)
-
-        def listing(row, carry):
-            filler.listing(row, row)
+        list_rows(filler, row_count)
+
+    @pl.when(pl.program_id(0) == pl.num_programs(0) - 1)
+    def _():
+        def outer(frame, carry):
+            for half in range(halves):
+                span = slice(half * lanes, (half + 1) * lanes)
+                for ref, row in ((first_ref, 0), (last_ref, row_count - 1)):
+                    ref[frame, :, span] = samples[
+                        frame, half, pl.ds(row, parts, stride=row_count), :
+                    ].astype(jnp.bfloat16)
             return carry
 
-        lax.fori_loop(0, row_count, listing, 0)
-
-    def rows(row, carry):
-        def fetch(entry, frame):
-            for half in range(halves):
-                filler.source[entry, :, half * lanes : (half + 1) * lanes] = samples[
-                    frame, half, pl.ds(row, parts, stride=row_count), :
-                ]
-
-        filler.row(row, row, fetch, (row + 2, row + 1, row))
-        return carry
-
-    def pack(index, carry):
-        devices, basis_count, stored, _ = out_ref.shape
-        pitch = row_count // pair
-        columns = stored // pitch
-        for v in range(basis_count):
-            turned = jnp.concatenate(
-                [filler.totals[pair * index + 1 + j, v] for j in range(pair)], axis=0
-            ).T
-            for d in range(devices):
-                out_ref[d, v, pl.ds(index, columns, stride=pitch), :] = turned[
-                    d * columns : (d + 1) * columns
-                ]
-        return carry
-
-    @pl.when(step == pl.num_programs(0) - 1)
-    def _():
-        lax.fori_loop(0, row_count, rows, 0)
-        lax.fori_loop(0, row_count // pair, pack, 0)
-
-
-def edge_kernel(
+        lax.fori_loop(0, frame_total, outer, 0)
+
+        def rows(index, carry):
+            add_row(filler, samples, row_count, index + quarter - 1)
+            return carry
+
+        lax.fori_loop(0, 2 * quarter + 2, rows, 0)
+        rest_ref[:2] = filler.totals[quarter - 1 : quarter + 1]
+        rest_ref[2:] = filler.totals[3 * quarter + 1 : 3 * quarter + 3]
+        pack_rows(filler, place_ref[0] // row_count, out_ref, lambda m: 2 * m + quarter)
+
+
+def outer_kernel(
     row_count,
     place_ref,
     pattern_ref,
     segment_ref,
     offset_ref,
     basis_ref,
+    block_ref,
+    kernel_ref,
+    rest_ref,
     low_ref,
     high_ref,
-    kernel_ref,
     out_ref,
+    samples,
     *scratch,
 ):
-    _, parts, kx_count = low_ref.shape
+    _, parts, _, kx_count = block_ref.shape
     refs = (place_ref, pattern_ref, segment_ref, offset_ref, basis_ref, kernel_ref)
     filler = Filler(refs, scratch, parts, kx_count)
-    filler.prepare((sublanes, lanes))
-    sides = ((-1, low_ref, (0, None, None)), (row_count, high_ref, (None, None, 1)))
-    for slot, (local, ref, targets) in enumerate(sides):
-        filler.listing(slot, local)
-
-        def fetch(entry, frame):
-            filler.source[entry] = ref[frame].astype(jnp.float32)
-
-        filler.row(slot, local, fetch, targets)
-    devices, basis_count, columns, _ = out_ref.shape
-    for v in range(basis_count):
-        turned = jnp.concatenate([filler.totals[0, v], filler.totals[1, v]], axis=0).T
-        for d in range(devices):
-            out_ref[d, v] = turned[d * columns : (d + 1) * columns]
-
-
-def image_kernel(row_count, coil_count, inverse_ref, block_ref, table_ref, out_ref, held):
-    devices, _, stored, _ = block_ref.shape
-    pair, part_count, length, width = held.shape
-    pitch = row_count // pair
-    columns = stored // pitch
+    quarter = row_count // 4
+    convert_frames(block_ref, samples)
+
+    @pl.when(pl.program_id(0) == 0)
+    def _():
+        filler.prepare((sublanes, lanes))
+        filler.totals[quarter - 1 : quarter + 1] = rest_ref[:2]
+        filler.totals[3 * quarter + 1 : 3 * quarter + 3] = rest_ref[2:]
+        list_rows(filler, row_count)
+
+    @pl.when(pl.program_id(0) == pl.num_programs(0) - 1)
+    def _():
+        def rows(index, carry):
+            beyond = (index >= quarter - 1).astype(jnp.int32)
+            add_row(filler, samples, row_count, index + beyond * (2 * quarter + 2))
+            return carry
+
+        lax.fori_loop(0, 2 * quarter - 2, rows, 0)
+
+        sides = (
+            (-1, low_ref, (1, None, None)),
+            (row_count, high_ref, (None, None, row_count)),
+        )
+        for local, ref, targets in sides:
+            filler.listing(0, local)
+
+            def fetch(entry, frame):
+                filler.source[entry] = ref[frame].astype(jnp.float32)
+
+            filler.row(0, local, fetch, targets)
+
+        def row_at(m):
+            return 2 * m + (2 * m >= quarter).astype(jnp.int32) * (2 * quarter)
+
+        pack_rows(filler, place_ref[0] // row_count, out_ref, row_at)
+
+
+def image_kernel(
+    row_count, coil_count, place_ref, inverse_ref, inner_ref, outer_ref, table_ref, out_ref, held
+):
+    devices, _, _, _ = inner_ref.shape
+    _, part_count, length, _ = held.shape
+    columns = length // coil_count
     parts = part_count * coil_count
     row_total = devices * row_count
+    own = place_ref[0] // row_count
     scale = inverse_ref[0:1, 0:1]
-    for x in range(columns):
-        turned = block_ref[:, 0, x * pitch : (x + 1) * pitch, :].reshape(width, lanes).T
-        for j in range(pair):
-            for p in range(part_count):
-                start = j * parts + p * coil_count
-                held[j, p, pl.ds(x, coil_count, stride=columns), :] = turned[
-                    start : start + coil_count
-                ]
+    for h, ref in enumerate((inner_ref, outer_ref)):
+        for i in range(sublanes):
+            turned = jnp.concatenate(
+                [ref[d ^ own, 0, i * sublanes : (i + 1) * sublanes, :] for d in range(devices)],
+                axis=0,
+            ).T
+            for j in range(columns // sublanes):
+                for p in range(part_count):
+                    start = j * parts + p * coil_count
+                    held[h, p, pl.ds(j * sublanes + i, coil_count, stride=columns), :] = turned[
+                        start : start + coil_count
+                    ]
     for start in range(0, length, lanes):
         left = jnp.concatenate(
-            [
-                held[j, p, start : start + lanes, :]
-                for p in range(part_count)
-                for j in range(pair)
-            ],
+            [held[h, p, start : start + lanes, :] for p in range(part_count) for h in range(2)],
             axis=1,
         )
         coarse = left.astype(jnp.bfloat16)
@@ -378,8 +449,10 @@
             out_ref[0, p, start : start + lanes, :] = result[:, p * row_total : (p + 1) * row_total]
 
 
-def inverse_table(row_total, pair):
-    row = np.arange(row_total).reshape(-1, pair).T.reshape(-1)
+def inverse_table(row_total, row_count):
+    quarter = row_count // 4
+    row = np.arange(row_total).reshape(-1, 4, quarter)
+    row = np.concatenate([row[:, 1:3].reshape(-1), row[:, 0::3].reshape(-1)])
     index = np.arange(row_total)
     angle = (row[:, None] * index[None, :] % row_total) * (2.0 * np.pi / row_total)
     cosine = np.cos(angle) / np.sqrt(row_total)
@@ -400,93 +473,110 @@
     fits = (
         2 * parts == lanes
         and row_count == 2 * sublanes
-        and columns % sublanes == 0
+        and columns == 2 * sublanes
         and row_total == 2 * lanes
         and kx_count % lanes == 0
         and tap_count * coil_count == lanes
         and frame_total % together == 0
+        and devices & (devices - 1) == 0
     )
     if not fits:
         return plain_device(kspace, kernel, pattern, offsets, segment, temporal_basis)
 
     basis_count = temporal_basis.shape[0]
     group_count = kernel.shape[0]
-    stored = columns * row_count // pair
+    stored = sublanes * row_count // 2
     halves = kx_count // lanes
-
-    forward = [(i, i + 1) for i in range(devices - 1)]
-    backward = [(i + 1, i) for i in range(devices - 1)]
     edge_shape = (frame_total, parts, kx_count)
-    low = lax.ppermute(kspace[:, :, :, -1, :].reshape(edge_shape), "ky", forward)
-    high = lax.ppermute(kspace[:, :, :, 0, :].reshape(edge_shape), "ky", backward)
+    payload_shape = (devices, basis_count, stored, lanes)
 
     place = (lax.axis_index("ky") * row_count).astype(jnp.int32).reshape(1)
     kernel_rows = kernel.transpose(0, 2, 1)
-    fill_work = 4 * frame_total * row_count * kx_count * kernel.shape[1] * parts
-
+    fill_work = 2 * frame_total * row_count * kx_count * kernel.shape[1] * parts
+    estimate = pl.CostEstimate(flops=fill_work, bytes_accessed=0, transcendentals=0)
+    scalars = (place, pattern, segment, offsets, temporal_basis)
+    samples = kspace.reshape(frame_total, parts, row_count, kx_count)
     scalar = pl.BlockSpec(memory_space=pltpu.SMEM)
 
-    def scratch(rows, slots):
-        return [
-            pltpu.VMEM((batch, parts, kx_count), jnp.float32),
-            pltpu.VMEM((batch, 2 * parts, kx_count), jnp.float32),
-            pltpu.VMEM((rows, basis_count, parts, kx_count), jnp.float32),
-            pltpu.VMEM((group_count, 3 * parts, tap_count * parts), jnp.bfloat16),
-            pltpu.SMEM((slots * frame_total + 1,), jnp.int32),
-            pltpu.SMEM((2 * slots,), jnp.int32),
-            pltpu.SMEM((1,), jnp.float32),
-        ]
-
-    scalars = (place, pattern, segment, offsets, temporal_basis)
-    payload, inverse = pl.pallas_call(
-        functools.partial(fill_kernel, row_count),
+    def whole(shape):
+        return pl.BlockSpec(shape, lambda t: (0,) * len(shape))
+
+    in_specs = [scalar] * len(scalars) + [
+        pl.BlockSpec((together, parts, row_count, kx_count), lambda t: (t, 0, 0, 0)),
+        whole(kernel_rows.shape),
+    ]
+    scratch_shapes = [
+        pltpu.VMEM((frame_total, halves, parts * row_count, lanes), jnp.float32),
+        pltpu.VMEM((batch, parts, kx_count), jnp.float32),
+        pltpu.VMEM((batch, 2 * parts, kx_count), jnp.float32),
+        pltpu.VMEM((row_count + 2, basis_count, parts, kx_count), jnp.float32),
+        pltpu.VMEM((group_count, 3 * parts, tap_count * parts), jnp.bfloat16),
+        pltpu.SMEM((row_count * frame_total + 1,), jnp.int32),
+        pltpu.SMEM((2 * row_count,), jnp.int32),
+        pltpu.SMEM((1,), jnp.float32),
+    ]
+    inner_shapes = [
+        jax.ShapeDtypeStruct(payload_shape, jnp.float32),
+        jax.ShapeDtypeStruct((sublanes, lanes), jnp.float32),
+        jax.ShapeDtypeStruct((4, basis_count, parts, kx_count), jnp.float32),
+        jax.ShapeDtypeStruct(edge_shape, jnp.bfloat16),
+        jax.ShapeDtypeStruct(edge_shape, jnp.bfloat16),
+    ]
+    inner, inverse, rest, first, last = pl.pallas_call(
+        functools.partial(inner_kernel, row_count),
         grid=(frame_total // together,),
-        in_specs=[scalar] * len(scalars)
-        + [
-            pl.BlockSpec((together, parts, row_count, kx_count), lambda t: (t, 0, 0, 0)),
-            pl.BlockSpec(kernel_rows.shape, lambda t: (0, 0, 0)),
-        ],
-        out_specs=[
-            pl.BlockSpec((devices, basis_count, stored, lanes), lambda t: (0, 0, 0, 0)),
-            pl.BlockSpec((sublanes, lanes), lambda t: (0, 0)),
-        ],
-        out_shape=[
-            jax.ShapeDtypeStruct((devices, basis_count, stored, lanes), jnp.float32),
-            jax.ShapeDtypeStruct((sublanes, lanes), jnp.float32),
-        ],
-        scratch_shapes=[
-            pltpu.VMEM((frame_total, halves, parts * row_count, lanes), jnp.float32)
-        ]
-        + scratch(row_count + 2, row_count),
-        cost_estimate=pl.CostEstimate(flops=fill_work, bytes_accessed=0, transcendentals=0),
-        name="fill",
-    )(*scalars, kspace.reshape(frame_total, parts, row_count, kx_count), kernel_rows)
-    whole = pl.BlockSpec(memory_space=pltpu.VMEM)
-    edges = pl.pallas_call(
-        functools.partial(edge_kernel, row_count),
-        in_specs=[scalar] * len(scalars) + [whole] * 3,
-        out_specs=whole,
-        out_shape=jax.ShapeDtypeStruct((devices, basis_count, columns, lanes), jnp.float32),
-        scratch_shapes=scratch(2, 2),
-        name="edge",
-    )(*scalars, low, high, kernel_rows)
-    spread = payload.reshape(devices, basis_count, columns, row_count // pair, lanes)
-    place_in = lax.broadcasted_iota(jnp.int32, spread.shape, 3)
-    lane = lax.broadcasted_iota(jnp.int32, spread.shape, 4)
-    outer = jnp.where(lane < parts, 0, row_count // pair - 1) == place_in
-    spread = spread + jnp.where(outer, edges[:, :, :, None, :], 0.0)
-    payload = spread.astype(jnp.float16).reshape(devices, basis_count, stored, lanes)
-    swapped = lax.all_to_all(
-        payload, "ky", split_axis=0, concat_axis=0, tiled=True
-    ).astype(jnp.float32)
-
-    table = jnp.asarray(inverse_table(row_total, pair))
+        in_specs=in_specs,
+        out_specs=[whole(shape.shape) for shape in inner_shapes],
+        out_shape=inner_shapes,
+        scratch_shapes=scratch_shapes,
+        cost_estimate=estimate,
+        name="inner",
+    )(*scalars, samples, kernel_rows)
+    low = lax.ppermute(last, "ky", [(i, i + 1) for i in range(devices - 1)])
+    high = lax.ppermute(first, "ky", [(i + 1, i) for i in range(devices - 1)])
+
+    def swap(block, distance):
+        return lax.ppermute(block, "ky", [(i, i ^ distance) for i in range(devices)])
+
+    chips = devices // 2
+
+    def paired(payload):
+        payload = payload.astype(jnp.float16)
+        partner = swap(payload[chips:], 1)
+        return [jnp.stack([payload[m], partner[m]]) for m in range(chips)]
+
+    def gathered(pairs, received):
+        return jnp.concatenate([pairs[0]] + received).astype(jnp.float32)
+
+    inner_pairs = paired(inner)
+    inner_pairs, held_place = lax.optimization_barrier((inner_pairs, place))
+    inner_received = []
+    for m in range(1, chips):
+        inner_received.append(swap(inner_pairs[m], 2 * m))
+    outer = pl.pallas_call(
+        functools.partial(outer_kernel, row_count),
+        grid=(frame_total // together,),
+        in_specs=in_specs + [whole(rest.shape), whole(edge_shape), whole(edge_shape)],
+        out_specs=whole(payload_shape),
+        out_shape=jax.ShapeDtypeStruct(payload_shape, jnp.float32),
+        scratch_shapes=scratch_shapes,
+        cost_estimate=estimate,
+        name="outer",
+    )(held_place, *scalars[1:], samples, kernel_rows, rest, low, high)
+    outer_pairs = paired(outer)
+    outer_received = [swap(outer_pairs[m], 2 * m) for m in range(1, chips)]
+    inner = gathered(inner_pairs, inner_received)
+    outer = gathered(outer_pairs, outer_received)
+
+    table = jnp.asarray(inverse_table(row_total, row_count))
     length = coil_count * columns
     images = pl.pallas_call(
         functools.partial(image_kernel, row_count, coil_count),
         grid=(basis_count,),
         in_specs=[
+            scalar,
             pl.BlockSpec((sublanes, lanes), lambda v: (0, 0)),
+            pl.BlockSpec((devices, 1, stored, lanes), lambda v: (0, v, 0, 0)),
             pl.BlockSpec((devices, 1, stored, lanes), lambda v: (0, v, 0, 0)),
             pl.BlockSpec(table.shape, lambda v: (0, 0, 0)),
         ],
@@ -495,10 +585,10 @@
             (basis_count, part_count, length, row_total), jnp.float32
         ),
         scratch_shapes=[
-            pltpu.VMEM((pair, part_count, length, row_total // pair), jnp.float32)
+            pltpu.VMEM((2, part_count, length, row_total // 2), jnp.float32)
         ],
         name="image",
-    )(inverse, swapped, table)
+    )(place, inverse, inner, outer, table)
     return images.reshape(basis_count, part_count, coil_count, columns, row_total)
 
 

time: 128 us -> 133 us (1.039)
  the two profiles are of different devices: /device:TPU:1 before, /device:TPU:10 now
where the time goes in v2:
time: 133 us; the launch traced here: 132 us
  Pallas kernels  46.8 us (35%)
  waiting for transfers between devices  42.4 us (32%)
  starting transfers between devices  31.7 us (24%)
  other arithmetic  8.44 us (6%)
  local copies, waits for them, and re-layouts  2.56 us (2%)
    ppermute x16, waiting for transfers between devices, swap(): lax.ppermute(block, 'ky', [(i, i ^ distance) for i in range(devices)])  35.1 us
    ppermute x16, starting transfers between devices, swap(): lax.ppermute(block, 'ky', [(i, i ^ distance) for i in range(devices)])  25.1 us
    pallas_call x1, Pallas kernels, on_device(): pl.pallas_call(functools.partial(inner_kernel, row_count), grid=(frame_to...  20.4 us
    pallas_call x1, Pallas kernels, on_device(): pl.pallas_call(functools.partial(outer_kernel, row_count), grid=(frame_to...  16.3 us
    pallas_call x1, Pallas kernels, on_device(): pl.pallas_call(functools.partial(image_kernel, row_count, coil_count), gr...  10 us
    ppermute x1, waiting for transfers between devices, on_device(): high = lax.ppermute(first, 'ky', [(i + 1, i) for i in range(devices - 1)])  6.76 us
    ppermute x1, starting transfers between devices, on_device(): high = lax.ppermute(first, 'ky', [(i + 1, i) for i in range(devices - 1)])  4.72 us
    convert_element_type x2, other arithmetic, paired(): payload = payload.astype(jnp.float16)  4.12 us
  transfers between devices with their start and end apart: 18, of which 10 were waited for; matrix products, arithmetic and copies ran while one was open for 4% of the time, Pallas kernels for 12%

profile of v2, /device:TPU:10, one launch (start us, length us, event | category | flops | bytes accessed | tf_op | source)
XLA Modules:
  0.0 132.2 jit_solution(15996715068458444918)
XLA Ops:
  0.0 20.4 %inner.1 = (f32[16,5,64,128]{3,2,1,0:T(8,128)}, f32[8,128]{1,0:T(8,128)}, f32[4,5,64,256]{3,2,1,0:T(8,128)}, bf16[16,64,256]{2,1,0:T(8,128)(2,1)}, bf16[16,64,256]{2,1,0:T(8,128)(2,1)}) custom-call(s32[1]{0:T(128)} %bitcast.place_ref, s32[16]{0:T(128)} %pattern_ref.3, s32[256]{0:T(256)} %segment_ref.3, s32[4]{0:T(128)} %offset_ref.3, f32[5,16]{1,0:T(8,128)} %basis_ref.3, ...), custom_call_target="tpu_custom_call" | custom-call | flops 6442450944 | tf_op jit(solution)/shard_map/inner/pallas_call | solution.py:525
  20.4 2.1 %convert_element_type.12 = f16[16,5,64,128]{3,2,1,0:T(8,128)(2,1)S(1)} convert(f32[16,5,64,128]{3,2,1,0:T(8,128)} %get-tuple-element.20) | non-fusion elementwise | flops 655360 | bytes 3932160 | tf_op jit(solution)/shard_map/convert_element_type | solution.py:544
  22.5 0.0 copy-start.2
  22.5 0.2 slice.137
  22.7 0.1 collective-permute-start
  22.8 0.8 copy-done.2
  23.5 1.9 %collective-permute-start.8 = (bf16[16,64,256]{2,1,0:T(8,128)(2,1)S(1)}, bf16[16,64,256]{2,1,0:T(8,128)(2,1)S(1)}, u32[]{:S(2)}, u32[]{:S(2)}) collective-permute-start(bf16[16,64,256]{2,1,0:T(8,128)(2,1)S(1)} %copy-done.2), channel_id=1, source_target_pairs={{0,1},{1,2},{2,3},{3,4},{4,5},{5,6},{6,7},{7,8},{8,9},{9,10},{10,1... | collective-permute-start | bytes 1572872 | tf_op jit(solution)/shard_map/ppermute | solution.py:535
  25.5 4.7 %collective-permute-start.9 = (bf16[16,64,256]{2,1,0:T(8,128)(2,1)S(1)}, bf16[16,64,256]{2,1,0:T(8,128)(2,1)S(1)}, u32[]{:S(2)}, u32[]{:S(2)}) collective-permute-start(bf16[16,64,256]{2,1,0:T(8,128)(2,1)S(1)} %copy-done), channel_id=1, source_target_pairs={{1,0},{2,1},{3,2},{4,3},{5,4},{6,5},{7,6},{8,7},{9,8},{10,9},{11,1... | collective-permute-start | bytes 1572872 | tf_op jit(solution)/shard_map/ppermute | solution.py:536
  30.2 0.2 fusion.1
  30.4 0.0 collective-permute-done
  30.4 0.2 fusion.3
  30.5 0.1 pad_maximum_fusion.6
  30.7 0.1 pad_maximum_fusion.4
  30.8 0.1 pad_maximum_fusion.2
  30.9 0.1 pad_maximum_fusion
  31.0 0.1 collective-permute-start.1
  31.1 0.6 collective-permute-start.2
  31.7 2.8 %collective-permute-start.3 = (f16[2,5,64,128]{3,2,1,0:T(8,128)(2,1)S(1)}, f16[2,5,64,128]{3,2,1,0:T(8,128)(2,1)S(1)}, u32[]{:S(2)}, u32[]{:S(2)}) collective-permute-start(f16[2,5,64,128]{3,2,1,0:T(8,128)(2,1)S(1)} %get-tuple-element.24), channel_id=1, source_target_pairs={{0,6},{1,7},{2,4},{3,5},{4,2},{5,3},{6,0},{7,1},{8,14},{9,15},{10,... | collective-permute-start | bytes 491528 | tf_op jit(solution)/shard_map/ppermute | solution.py:539
  34.5 0.5 collective-permute-done.8.low_ref
  35.0 2.4 %collective-permute-start.4 = (f16[2,5,64,128]{3,2,1,0:T(8,128)(2,1)S(1)}, f16[2,5,64,128]{3,2,1,0:T(8,128)(2,1)S(1)}, u32[]{:S(2)}, u32[]{:S(2)}) collective-permute-start(f16[2,5,64,128]{3,2,1,0:T(8,128)(2,1)S(1)} %get-tuple-element.25), channel_id=1, source_target_pairs={{0,8},{1,9},{2,10},{3,11},{4,12},{5,13},{6,14},{7,15},{8,0},{9,1},... | collective-permute-start | bytes 491528 | tf_op jit(solution)/shard_map/ppermute | solution.py:539
  37.4 6.8 %collective-permute-done.9.high_ref = bf16[16,64,256]{2,1,0:T(8,128)(2,1)S(1)} collective-permute-done((bf16[16,64,256]{2,1,0:T(8,128)(2,1)S(1)}, bf16[16,64,256]{2,1,0:T(8,128)(2,1)S(1)}, u32[]{:S(2)}, u32[]{:S(2)}) %collective-permute-start.9) | collective-permute-done | bytes 524320 | tf_op jit(solution)/shard_map/ppermute | solution.py:536
  44.2 3.0 %collective-permute-start.5 = (f16[2,5,64,128]{3,2,1,0:T(8,128)(2,1)S(1)}, f16[2,5,64,128]{3,2,1,0:T(8,128)(2,1)S(1)}, u32[]{:S(2)}, u32[]{:S(2)}) collective-permute-start(f16[2,5,64,128]{3,2,1,0:T(8,128)(2,1)S(1)} %get-tuple-element.26), channel_id=1, source_target_pairs={{0,10},{1,11},{2,8},{3,9},{4,14},{5,15},{6,12},{7,13},{8,2},{9,3},... | collective-permute-start | bytes 491528 | tf_op jit(solution)/shard_map/ppermute | solution.py:539
  47.2 16.3 %outer.1 = f32[16,5,64,128]{3,2,1,0:T(8,128)} custom-call(s32[1]{0:T(128)} %bitcast.place_ref, s32[16]{0:T(128)} %pattern_ref.3, s32[256]{0:T(256)} %segment_ref.3, s32[4]{0:T(128)} %offset_ref.3, f32[5,16]{1,0:T(8,128)} %basis_ref.3, bf16[16,64,16,256]{3,2,1,0:T(8,128)(2,1)} %bitcast.5, bf16[2,64,768]{2,1,0:T(8,128)(2,1)} %bitcast.7, ...), custom_call_target="tpu_custom_call" | custom-call | flops 6442450944 | tf_op jit(solution)/shard_map/outer/pallas_call | solution.py:556
  63.5 2.1 %convert_element_type.14 = f16[16,5,64,128]{3,2,1,0:T(8,128)(2,1)S(1)} convert(f32[16,5,64,128]{3,2,1,0:T(8,128)} %outer.1) | non-fusion elementwise | flops 655360 | bytes 3932160 | tf_op jit(solution)/shard_map/convert_element_type | solution.py:544
  65.6 0.2 fusion
  65.8 0.2 slice.154
  66.0 0.0 collective-permute-done.1
  66.0 0.1 collective-permute-start.6
  66.1 0.1 constant_dynamic-update-slice_fusion.6
  66.2 0.0 collective-permute-done.2
  66.2 2.2 %collective-permute-start.10 = (f16[8,5,64,128]{3,2,1,0:T(8,128)(2,1)S(1)}, f16[8,5,64,128]{3,2,1,0:T(8,128)(2,1)S(1)}, u32[]{:S(2)}, u32[]{:S(2)}) collective-permute-start(f16[8,5,64,128]{3,2,1,0:T(8,128)(2,1)S(1)} %slice.154), channel_id=1, source_target_pairs={{0,1},{1,0},{2,3},{3,2},{4,5},{5,4},{6,7},{7,6},{8,9},{9,8},{10,11... | collective-permute-start | bytes 1966088 | tf_op jit(solution)/shard_map/ppermute | solution.py:539
  68.4 0.0 collective-permute-done.3
  68.4 2.2 %collective-permute-start.7 = (f16[2,5,64,128]{3,2,1,0:T(8,128)(2,1)S(1)}, f16[2,5,64,128]{3,2,1,0:T(8,128)(2,1)S(1)}, u32[]{:S(2)}, u32[]{:S(2)}) collective-permute-start(f16[2,5,64,128]{3,2,1,0:T(8,128)(2,1)S(1)} %get-tuple-element.28), channel_id=1, source_target_pairs={{0,14},{1,15},{2,12},{3,13},{4,10},{5,11},{6,8},{7,9},{8,6},{9,7},... | collective-permute-start | bytes 491528 | tf_op jit(solution)/shard_map/ppermute | solution.py:539
  70.7 0.0 collective-permute-done.4
  70.7 0.1 constant_dynamic-update-slice_fusion.3
  70.8 0.0 collective-permute-done.5
  70.8 0.1 constant_dynamic-update-slice_fusion.2
  70.8 9.4 %collective-permute-done.6 = f16[2,5,64,128]{3,2,1,0:T(8,128)(2,1)S(1)} collective-permute-done((f16[2,5,64,128]{3,2,1,0:T(8,128)(2,1)S(1)}, f16[2,5,64,128]{3,2,1,0:T(8,128)(2,1)S(1)}, u32[]{:S(2)}, u32[]{:S(2)}) %collective-permute-start.6) | collective-permute-done | bytes 163872 | tf_op jit(solution)/shard_map/ppermute | solution.py:539
  80.2 1.9 %collective-permute-done.7 = f16[2,5,64,128]{3,2,1,0:T(8,128)(2,1)S(1)} collective-permute-done((f16[2,5,64,128]{3,2,1,0:T(8,128)(2,1)S(1)}, f16[2,5,64,128]{3,2,1,0:T(8,128)(2,1)S(1)}, u32[]{:S(2)}, u32[]{:S(2)}) %collective-permute-start.7) | collective-permute-done | bytes 163872 | tf_op jit(solution)/shard_map/ppermute | solution.py:539
  82.2 1.8 %convert_element_type.13.inner_ref = f32[16,5,64,128]{3,2,1,0:T(8,128)} convert(f16[16,5,64,128]{3,2,1,0:T(8,128)(2,1)S(1)} %constant_dynamic-update-slice_fusion) | non-fusion elementwise | flops 655360 | bytes 3932160 | tf_op jit(solution)/shard_map/convert_element_type | solution.py:549
  84.0 0.0 collective-permute-done.10
  84.0 0.2 fusion.2
  84.2 0.1 pad_maximum_fusion.8
  84.2 3.1 %collective-permute-start.11 = (f16[2,5,64,128]{3,2,1,0:T(8,128)(2,1)S(1)}, f16[2,5,64,128]{3,2,1,0:T(8,128)(2,1)S(1)}, u32[]{:S(2)}, u32[]{:S(2)}) collective-permute-start(f16[2,5,64,128]{3,2,1,0:T(8,128)(2,1)S(1)} %pad_maximum_fusion.8), channel_id=1, source_target_pairs={{0,2},{1,3},{2,0},{3,1},{4,6},{5,7},{6,4},{7,5},{8,10},{9,11},{10,... | collective-permute-start | bytes 491528 | tf_op jit(solution)/shard_map/ppermute | solution.py:539
  87.4 0.1 collective-permute-start.12
  87.5 1.5 %collective-permute-start.13 = (f16[2,5,64,128]{3,2,1,0:T(8,128)(2,1)S(1)}, f16[2,5,64,128]{3,2,1,0:T(8,128)(2,1)S(1)}, u32[]{:S(2)}, u32[]{:S(2)}) collective-permute-start(f16[2,5,64,128]{3,2,1,0:T(8,128)(2,1)S(1)} %pad_maximum_fusion.10), channel_id=1, source_target_pairs={{0,6},{1,7},{2,4},{3,5},{4,2},{5,3},{6,0},{7,1},{8,14},{9,15},{10,... | collective-permute-start | bytes 491528 | tf_op jit(solution)/shard_map/ppermute | solution.py:539
  89.1 1.9 %collective-permute-start.14 = (f16[2,5,64,128]{3,2,1,0:T(8,128)(2,1)S(1)}, f16[2,5,64,128]{3,2,1,0:T(8,128)(2,1)S(1)}, u32[]{:S(2)}, u32[]{:S(2)}) collective-permute-start(f16[2,5,64,128]{3,2,1,0:T(8,128)(2,1)S(1)} %pad_maximum_fusion.11), channel_id=1, source_target_pairs={{0,8},{1,9},{2,10},{3,11},{4,12},{5,13},{6,14},{7,15},{8,0},{9,1},... | collective-permute-start | bytes 491528 | tf_op jit(solution)/shard_map/ppermute | solution.py:539
  91.1 2.6 %collective-permute-start.15 = (f16[2,5,64,128]{3,2,1,0:T(8,128)(2,1)S(1)}, f16[2,5,64,128]{3,2,1,0:T(8,128)(2,1)S(1)}, u32[]{:S(2)}, u32[]{:S(2)}) collective-permute-start(f16[2,5,64,128]{3,2,1,0:T(8,128)(2,1)S(1)} %pad_maximum_fusion.12), channel_id=1, source_target_pairs={{0,10},{1,11},{2,8},{3,9},{4,14},{5,15},{6,12},{7,13},{8,2},{9,3},... | collective-permute-start | bytes 491528 | tf_op jit(solution)/shard_map/ppermute | solution.py:539
  93.7 0.0 collective-permute-done.11
  93.7 0.5 collective-permute-start.16
  94.2 0.1 constant_dynamic-update-slice_fusion.14
  94.3 3.0 %collective-permute-done.12 = f16[2,5,64,128]{3,2,1,0:T(8,128)(2,1)S(1)} collective-permute-done((f16[2,5,64,128]{3,2,1,0:T(8,128)(2,1)S(1)}, f16[2,5,64,128]{3,2,1,0:T(8,128)(2,1)S(1)}, u32[]{:S(2)}, u32[]{:S(2)}) %collective-permute-start.12) | collective-permute-done | bytes 163872 | tf_op jit(solution)/shard_map/ppermute | solution.py:539
  97.3 1.9 %collective-permute-start.17 = (f16[2,5,64,128]{3,2,1,0:T(8,128)(2,1)S(1)}, f16[2,5,64,128]{3,2,1,0:T(8,128)(2,1)S(1)}, u32[]{:S(2)}, u32[]{:S(2)}) collective-permute-start(f16[2,5,64,128]{3,2,1,0:T(8,128)(2,1)S(1)} %pad_maximum_fusion.14), channel_id=1, source_target_pairs={{0,14},{1,15},{2,12},{3,13},{4,10},{5,11},{6,8},{7,9},{8,6},{9,7},... | collective-permute-start | bytes 491528 | tf_op jit(solution)/shard_map/ppermute | solution.py:539
  99.2 0.1 constant_dynamic-update-slice_fusion.13
  99.2 0.8 collective-permute-done.13
  100.1 0.1 constant_dynamic-update-slice_fusion.12
  100.1 1.3 %collective-permute-done.14 = f16[2,5,64,128]{3,2,1,0:T(8,128)(2,1)S(1)} collective-permute-done((f16[2,5,64,128]{3,2,1,0:T(8,128)(2,1)S(1)}, f16[2,5,64,128]{3,2,1,0:T(8,128)(2,1)S(1)}, u32[]{:S(2)}, u32[]{:S(2)}) %collective-permute-start.14) | collective-permute-done | bytes 163872 | tf_op jit(solution)/shard_map/ppermute | solution.py:539
  101.5 0.1 constant_dynamic-update-slice_fusion.11
  101.5 11.1 %collective-permute-done.15 = f16[2,5,64,128]{3,2,1,0:T(8,128)(2,1)S(1)} collective-permute-done((f16[2,5,64,128]{3,2,1,0:T(8,128)(2,1)S(1)}, f16[2,5,64,128]{3,2,1,0:T(8,128)(2,1)S(1)}, u32[]{:S(2)}, u32[]{:S(2)}) %collective-permute-start.15) | collective-permute-done | bytes 163872 | tf_op jit(solution)/shard_map/ppermute | solution.py:539
  112.7 0.1 constant_dynamic-update-slice_fusion.10
  112.7 4.6 %collective-permute-done.16 = f16[2,5,64,128]{3,2,1,0:T(8,128)(2,1)S(1)} collective-permute-done((f16[2,5,64,128]{3,2,1,0:T(8,128)(2,1)S(1)}, f16[2,5,64,128]{3,2,1,0:T(8,128)(2,1)S(1)}, u32[]{:S(2)}, u32[]{:S(2)}) %collective-permute-start.16) | collective-permute-done | bytes 163872 | tf_op jit(solution)/shard_map/ppermute | solution.py:539
  117.4 2.9 %collective-permute-done.17 = f16[2,5,64,128]{3,2,1,0:T(8,128)(2,1)S(1)} collective-permute-done((f16[2,5,64,128]{3,2,1,0:T(8,128)(2,1)S(1)}, f16[2,5,64,128]{3,2,1,0:T(8,128)(2,1)S(1)}, u32[]{:S(2)}, u32[]{:S(2)}) %collective-permute-start.17) | collective-permute-done | bytes 163872 | tf_op jit(solution)/shard_map/ppermute | solution.py:539
  120.4 1.8 %convert_element_type.15.outer_ref = f32[16,5,64,128]{3,2,1,0:T(8,128)} convert(f16[16,5,64,128]{3,2,1,0:T(8,128)(2,1)S(1)} %constant_dynamic-update-slice_fusion.8) | non-fusion elementwise | flops 655360 | bytes 3932160 | tf_op jit(solution)/shard_map/convert_element_type | solution.py:549
  122.2 10.0 %image.1 = f32[5,2,512,256]{3,2,1,0:T(8,128)} custom-call(s32[1]{0:T(128)} %bitcast.place_ref, f32[8,128]{1,0:T(8,128)} %get-tuple-element.19.inverse_ref, f32[16,5,64,128]{3,2,1,0:T(8,128)} %convert_element_type.13.inner_ref, f32[16,5,64,128]{3,2,1,0:T(8,128)} %convert_element_type.15.outer_ref, bf16[2,512,512]{2,1,0:T(8,128)(2,1)} %constant.8.clone.table_ref), custom_call_target="tpu_custom_call" | custom-call | tf_op jit(solution)/shard_map/image/pallas_call | solution.py:573
  (19 shorter events, 0.6 us)
Async XLA Ops:
  22.5 1.0 copy-start.2
  22.5 3.0 %copy-start = (bf16[16,64,256]{2,1,0:T(8,128)(2,1)S(1)}, bf16[16,64,256]{2,1,0:T(8,128)(2,1)}, u32[]{:S(2)}) copy-start(bf16[16,64,256]{2,1,0:T(8,128)(2,1)} %get-tuple-element.32) | copy-start | bytes 1572868
  22.7 7.7 %collective-permute-start = (f16[8,5,64,128]{3,2,1,0:T(8,128)(2,1)S(1)}, f16[8,5,64,128]{3,2,1,0:T(8,128)(2,1)S(1)}, u32[]{:S(2)}, u32[]{:S(2)}) collective-permute-start(f16[8,5,64,128]{3,2,1,0:T(8,128)(2,1)S(1)} %slice.137), channel_id=1, source_target_pairs={{0,1},{1,0},{2,3},{3,2},{4,5},{5,4},{6,7},{7,6},{8,9},{9,8},{10,11... | collective-permute-start | bytes 1966088 | tf_op jit(solution)/shard_map/ppermute | solution.py:539
  23.5 11.5 %collective-permute-start.8 = (bf16[16,64,256]{2,1,0:T(8,128)(2,1)S(1)}, bf16[16,64,256]{2,1,0:T(8,128)(2,1)S(1)}, u32[]{:S(2)}, u32[]{:S(2)}) collective-permute-start(bf16[16,64,256]{2,1,0:T(8,128)(2,1)S(1)} %copy-done.2), channel_id=1, source_target_pairs={{0,1},{1,2},{2,3},{3,4},{4,5},{5,6},{6,7},{7,8},{8,9},{9,10},{10,1... | collective-permute-start | bytes 1572872 | tf_op jit(solution)/shard_map/ppermute | solution.py:535
  25.5 18.7 %collective-permute-start.9 = (bf16[16,64,256]{2,1,0:T(8,128)(2,1)S(1)}, bf16[16,64,256]{2,1,0:T(8,128)(2,1)S(1)}, u32[]{:S(2)}, u32[]{:S(2)}) collective-permute-start(bf16[16,64,256]{2,1,0:T(8,128)(2,1)S(1)} %copy-done), channel_id=1, source_target_pairs={{1,0},{2,1},{3,2},{4,3},{5,4},{6,5},{7,6},{8,7},{9,8},{10,9},{11,1... | collective-permute-start | bytes 1572872 | tf_op jit(solution)/shard_map/ppermute | solution.py:536
  31.0 35.0 %collective-permute-start.1 = (f16[2,5,64,128]{3,2,1,0:T(8,128)(2,1)S(1)}, f16[2,5,64,128]{3,2,1,0:T(8,128)(2,1)S(1)}, u32[]{:S(2)}, u32[]{:S(2)}) collective-permute-start(f16[2,5,64,128]{3,2,1,0:T(8,128)(2,1)S(1)} %get-tuple-element.22), channel_id=1, source_target_pairs={{0,2},{1,3},{2,0},{3,1},{4,6},{5,7},{6,4},{7,5},{8,10},{9,11},{10,... | collective-permute-start | bytes 491528 | tf_op jit(solution)/shard_map/ppermute | solution.py:539
  31.1 35.1 %collective-permute-start.2 = (f16[2,5,64,128]{3,2,1,0:T(8,128)(2,1)S(1)}, f16[2,5,64,128]{3,2,1,0:T(8,128)(2,1)S(1)}, u32[]{:S(2)}, u32[]{:S(2)}) collective-permute-start(f16[2,5,64,128]{3,2,1,0:T(8,128)(2,1)S(1)} %get-tuple-element.23), channel_id=1, source_target_pairs={{0,4},{1,5},{2,6},{3,7},{4,0},{5,1},{6,2},{7,3},{8,12},{9,13},{10,... | collective-permute-start | bytes 491528 | tf_op jit(solution)/shard_map/ppermute | solution.py:539
  31.7 36.7 %collective-permute-start.3 = (f16[2,5,64,128]{3,2,1,0:T(8,128)(2,1)S(1)}, f16[2,5,64,128]{3,2,1,0:T(8,128)(2,1)S(1)}, u32[]{:S(2)}, u32[]{:S(2)}) collective-permute-start(f16[2,5,64,128]{3,2,1,0:T(8,128)(2,1)S(1)} %get-tuple-element.24), channel_id=1, source_target_pairs={{0,6},{1,7},{2,4},{3,5},{4,2},{5,3},{6,0},{7,1},{8,14},{9,15},{10,... | collective-permute-start | bytes 491528 | tf_op jit(solution)/shard_map/ppermute | solution.py:539
  35.0 12.2 %copy-start.1 = (bf16[16,64,256]{2,1,0:T(8,128)(2,1)}, bf16[16,64,256]{2,1,0:T(8,128)(2,1)S(1)}, u32[]{:S(2)}) copy-start(bf16[16,64,256]{2,1,0:T(8,128)(2,1)S(1)} %collective-permute-done.8.low_ref) | copy-start | bytes 1572868
  35.0 35.7 %collective-permute-start.4 = (f16[2,5,64,128]{3,2,1,0:T(8,128)(2,1)S(1)}, f16[2,5,64,128]{3,2,1,0:T(8,128)(2,1)S(1)}, u32[]{:S(2)}, u32[]{:S(2)}) collective-permute-start(f16[2,5,64,128]{3,2,1,0:T(8,128)(2,1)S(1)} %get-tuple-element.25), channel_id=1, source_target_pairs={{0,8},{1,9},{2,10},{3,11},{4,12},{5,13},{6,14},{7,15},{8,0},{9,1},... | collective-permute-start | bytes 491528 | tf_op jit(solution)/shard_map/ppermute | solution.py:539
  44.2 3.0 %copy-start.3 = (bf16[16,64,256]{2,1,0:T(8,128)(2,1)}, bf16[16,64,256]{2,1,0:T(8,128)(2,1)S(1)}, u32[]{:S(2)}) copy-start(bf16[16,64,256]{2,1,0:T(8,128)(2,1)S(1)} %collective-permute-done.9.high_ref) | copy-start | bytes 1572868
  44.2 26.6 %collective-permute-start.5 = (f16[2,5,64,128]{3,2,1,0:T(8,128)(2,1)S(1)}, f16[2,5,64,128]{3,2,1,0:T(8,128)(2,1)S(1)}, u32[]{:S(2)}, u32[]{:S(2)}) collective-permute-start(f16[2,5,64,128]{3,2,1,0:T(8,128)(2,1)S(1)} %get-tuple-element.26), channel_id=1, source_target_pairs={{0,10},{1,11},{2,8},{3,9},{4,14},{5,15},{6,12},{7,13},{8,2},{9,3},... | collective-permute-start | bytes 491528 | tf_op jit(solution)/shard_map/ppermute | solution.py:539
  66.0 14.2 %collective-permute-start.6 = (f16[2,5,64,128]{3,2,1,0:T(8,128)(2,1)S(1)}, f16[2,5,64,128]{3,2,1,0:T(8,128)(2,1)S(1)}, u32[]{:S(2)}, u32[]{:S(2)}) collective-permute-start(f16[2,5,64,128]{3,2,1,0:T(8,128)(2,1)S(1)} %get-tuple-element.27), channel_id=1, source_target_pairs={{0,12},{1,13},{2,14},{3,15},{4,8},{5,9},{6,10},{7,11},{8,4},{9,5},... | collective-permute-start | bytes 491528 | tf_op jit(solution)/shard_map/ppermute | solution.py:539
  66.2 17.8 %collective-permute-start.10 = (f16[8,5,64,128]{3,2,1,0:T(8,128)(2,1)S(1)}, f16[8,5,64,128]{3,2,1,0:T(8,128)(2,1)S(1)}, u32[]{:S(2)}, u32[]{:S(2)}) collective-permute-start(f16[8,5,64,128]{3,2,1,0:T(8,128)(2,1)S(1)} %slice.154), channel_id=1, source_target_pairs={{0,1},{1,0},{2,3},{3,2},{4,5},{5,4},{6,7},{7,6},{8,9},{9,8},{10,11... | collective-permute-start | bytes 1966088 | tf_op jit(solution)/shard_map/ppermute | solution.py:539
  68.4 13.7 %collective-permute-start.7 = (f16[2,5,64,128]{3,2,1,0:T(8,128)(2,1)S(1)}, f16[2,5,64,128]{3,2,1,0:T(8,128)(2,1)S(1)}, u32[]{:S(2)}, u32[]{:S(2)}) collective-permute-start(f16[2,5,64,128]{3,2,1,0:T(8,128)(2,1)S(1)} %get-tuple-element.28), channel_id=1, source_target_pairs={{0,14},{1,15},{2,12},{3,13},{4,10},{5,11},{6,8},{7,9},{8,6},{9,7},... | collective-permute-start | bytes 491528 | tf_op jit(solution)/shard_map/ppermute | solution.py:539
  84.2 9.5 %collective-permute-start.11 = (f16[2,5,64,128]{3,2,1,0:T(8,128)(2,1)S(1)}, f16[2,5,64,128]{3,2,1,0:T(8,128)(2,1)S(1)}, u32[]{:S(2)}, u32[]{:S(2)}) collective-permute-start(f16[2,5,64,128]{3,2,1,0:T(8,128)(2,1)S(1)} %pad_maximum_fusion.8), channel_id=1, source_target_pairs={{0,2},{1,3},{2,0},{3,1},{4,6},{5,7},{6,4},{7,5},{8,10},{9,11},{10,... | collective-permute-start | bytes 491528 | tf_op jit(solution)/shard_map/ppermute | solution.py:539
  87.4 9.9 %collective-permute-start.12 = (f16[2,5,64,128]{3,2,1,0:T(8,128)(2,1)S(1)}, f16[2,5,64,128]{3,2,1,0:T(8,128)(2,1)S(1)}, u32[]{:S(2)}, u32[]{:S(2)}) collective-permute-start(f16[2,5,64,128]{3,2,1,0:T(8,128)(2,1)S(1)} %pad_maximum_fusion.9), channel_id=1, source_target_pairs={{0,4},{1,5},{2,6},{3,7},{4,0},{5,1},{6,2},{7,3},{8,12},{9,13},{10,... | collective-permute-start | bytes 491528 | tf_op jit(solution)/shard_map/ppermute | solution.py:539
  87.5 12.6 %collective-permute-start.13 = (f16[2,5,64,128]{3,2,1,0:T(8,128)(2,1)S(1)}, f16[2,5,64,128]{3,2,1,0:T(8,128)(2,1)S(1)}, u32[]{:S(2)}, u32[]{:S(2)}) collective-permute-start(f16[2,5,64,128]{3,2,1,0:T(8,128)(2,1)S(1)} %pad_maximum_fusion.10), channel_id=1, source_target_pairs={{0,6},{1,7},{2,4},{3,5},{4,2},{5,3},{6,0},{7,1},{8,14},{9,15},{10,... | collective-permute-start | bytes 491528 | tf_op jit(solution)/shard_map/ppermute | solution.py:539
  89.1 12.4 %collective-permute-start.14 = (f16[2,5,64,128]{3,2,1,0:T(8,128)(2,1)S(1)}, f16[2,5,64,128]{3,2,1,0:T(8,128)(2,1)S(1)}, u32[]{:S(2)}, u32[]{:S(2)}) collective-permute-start(f16[2,5,64,128]{3,2,1,0:T(8,128)(2,1)S(1)} %pad_maximum_fusion.11), channel_id=1, source_target_pairs={{0,8},{1,9},{2,10},{3,11},{4,12},{5,13},{6,14},{7,15},{8,0},{9,1},... | collective-permute-start | bytes 491528 | tf_op jit(solution)/shard_map/ppermute | solution.py:539
  91.1 21.6 %collective-permute-start.15 = (f16[2,5,64,128]{3,2,1,0:T(8,128)(2,1)S(1)}, f16[2,5,64,128]{3,2,1,0:T(8,128)(2,1)S(1)}, u32[]{:S(2)}, u32[]{:S(2)}) collective-permute-start(f16[2,5,64,128]{3,2,1,0:T(8,128)(2,1)S(1)} %pad_maximum_fusion.12), channel_id=1, source_target_pairs={{0,10},{1,11},{2,8},{3,9},{4,14},{5,15},{6,12},{7,13},{8,2},{9,3},... | collective-permute-start | bytes 491528 | tf_op jit(solution)/shard_map/ppermute | solution.py:539
  93.7 23.6 %collective-permute-start.16 = (f16[2,5,64,128]{3,2,1,0:T(8,128)(2,1)S(1)}, f16[2,5,64,128]{3,2,1,0:T(8,128)(2,1)S(1)}, u32[]{:S(2)}, u32[]{:S(2)}) collective-permute-start(f16[2,5,64,128]{3,2,1,0:T(8,128)(2,1)S(1)} %pad_maximum_fusion.13), channel_id=1, source_target_pairs={{0,12},{1,13},{2,14},{3,15},{4,8},{5,9},{6,10},{7,11},{8,4},{9,5},... | collective-permute-start | bytes 491528 | tf_op jit(solution)/shard_map/ppermute | solution.py:539
  97.3 23.1 %collective-permute-start.17 = (f16[2,5,64,128]{3,2,1,0:T(8,128)(2,1)S(1)}, f16[2,5,64,128]{3,2,1,0:T(8,128)(2,1)S(1)}, u32[]{:S(2)}, u32[]{:S(2)}) collective-permute-start(f16[2,5,64,128]{3,2,1,0:T(8,128)(2,1)S(1)} %pad_maximum_fusion.14), channel_id=1, source_target_pairs={{0,14},{1,15},{2,12},{3,13},{4,10},{5,11},{6,8},{7,9},{8,6},{9,7},... | collective-permute-start | bytes 491528 | tf_op jit(solution)/shard_map/ppermute | solution.py:539
